TPU v7x, 768 devices: a whole 4x8x12 slice. The times are simulated.
768 devices in a mesh: aa: 12 (over z), ba: 64 (over y, x, core).
Axes of the slice: x: 4, y: 8, z: 12, core: 2. Of those that a mesh axis runs over, the one named last changes fastest.
Arguments:
- grad_out: bfloat16 [98304, 4096], P('aa', 'ba')
- saved_input: bfloat16 [98304, 4096], P(('aa', 'ba'))
- keep_bits: int32 [98304, 128], P(('aa', 'ba')), may hold values from -2147483648 to 2147483647, as said below
- gain: float32 [4096], replicated, may hold values from 0.5 to 1.5
Outputs:
- grad_in: bfloat16 [98304, 4096], P(('aa', 'ba'))
- gain_grad: float32 [4096], P('ba')
Inputs may be any that keep to these rules, and one draw needn't show every extreme that they name: `keep_bits`: bit k of word w in row t (bit 31 being the sign bit) is the keep flag of feature 32 * w + k of token t; about nine in ten flags are 1.
All inputs are finite; a program needn't handle non-finite values.
Results may differ from a plain program's by a relative error of at most 0.001.
Values may be sent and summed in bfloat16 or wider, within the bound.
No kernel may reach another device: no remote copies, remote signals or barrier semaphores. Data moves between devices by JAX's collectives and lax.ppermute only.
A program may use at most 32 MiB of HBM per device.

v0:
```python
import math

import jax
import jax.numpy as jnp
from jax import lax
from jax.sharding import PartitionSpec as P

KEEP_RATE = 0.9
EPSILON = 1e-06


def split_up(value, dim, devices):
    before, after = (value.shape[:dim], value.shape[dim + 1 :])
    return jnp.moveaxis(value.reshape(*before, devices, -1, *after), dim, 0)


def sum_at_owner(value, axis, dim):
    parts = split_up(value, dim, lax.axis_size(axis))
    arrived = lax.all_to_all(parts, axis, split_axis=0, concat_axis=0, tiled=True)
    return arrived.sum(axis=0)


def from_everyone(value, axis):
    devices = lax.axis_size(axis)
    return lax.all_to_all(
        jnp.broadcast_to(value[None], (devices, *value.shape)), axis, 0, 0, tiled=True
    )


def over_copies(value, axis):
    everything = from_everyone(value, axis)
    return jnp.sum(everything, axis=0)


def unpack_bits(words):
    shifts = jnp.arange(32, dtype=jnp.int32)
    bits = jnp.right_shift(words[:, :, None], shifts[None, None, :]) & 1
    return bits.reshape(words.shape[0], words.shape[1] * 32).astype(jnp.float32)


def rows_backward(grad_rows, input_rows, word_rows, gain):
    keep = unpack_bits(word_rows)
    dropped = input_rows.astype(jnp.float32) * keep * (1.0 / KEEP_RATE)
    inverse = lax.rsqrt(jnp.mean(dropped * dropped, axis=-1, keepdims=True) + EPSILON)
    normed = dropped * inverse
    grads = grad_rows.astype(jnp.float32)
    scaled = gain[None, :] * grads
    centre = jnp.mean(scaled * normed, axis=-1, keepdims=True)
    grad_in = (inverse * (scaled - normed * centre) * keep * (1.0 / KEEP_RATE)).astype(jnp.bfloat16)
    partial_sum = jnp.sum(grads * normed, axis=0)
    return (grad_in, partial_sum)


def per_device(grad_out, saved_input, keep_bits, gain):
    groups = lax.axis_size("ba")
    rows = grad_out.shape[0] // groups
    pieces = grad_out.reshape(groups, rows, grad_out.shape[1])
    arrived = lax.all_to_all(pieces, "ba", split_axis=0, concat_axis=2, tiled=True)
    grad_rows = arrived.reshape(rows, arrived.shape[2])
    grad_in, partial_sum = rows_backward(grad_rows, saved_input, keep_bits, gain)
    total_tokens = rows * groups * lax.axis_size("aa")
    owned = sum_at_owner(partial_sum, "ba", 0)
    share = over_copies(owned, "aa")
    gain_grad = share * (1.0 / math.sqrt(total_tokens))
    return (grad_in, gain_grad)


def solution(mesh):
    placed = (P("aa", "ba"), P(("aa", "ba"), None), P(("aa", "ba"), None), P())
    return jax.shard_map(
        per_device,
        mesh=mesh,
        in_specs=placed,
        out_specs=(P(("aa", "ba"), None), P("ba")),
        check_vma=False,
    )
```

profile of v0, /device:TPU:1, one launch (start us, length us, event | category | flops | bytes accessed | tf_op | source)
XLA Modules:
  0.0 85.5 jit_solution(15992088605288349493)
XLA Ops:
  0.6 0.0 copy-start
  0.6 1.2 %copy-done = bf16[8192,64]{0,1:T(8,128)(2,1)S(1)} copy-done((bf16[8192,64]{0,1:T(8,128)(2,1)S(1)}, bf16[8192,64]{0,1:T(8,128)(2,1)}, u32[]{:S(2)}) %copy-start) | copy-done | bytes 1048600
  1.9 1.3 %copy_bitcast_fusion = bf16[64,128,64]{1,2,0:T(8,128)(2,1)} fusion(bf16[8192,64]{0,1:T(8,128)(2,1)S(1)} %copy-done), kind=kLoop, calls=%fused_computation.16 | loop fusion | bytes 2097152 | tf_op jit(solution)/shard_map/reshape | solution.py:57
  3.1 14.6 %all-to-all-start = ((bf16[64,128,64]{1,2,0:T(8,128)(2,1)}), bf16[64,128,64]{1,2,0:T(8,128)(2,1)S(1)}, u32[]{:S(2)}, u32[]{:S(2)}) async-start(bf16[64,128,64]{1,2,0:T(8,128)(2,1)} %copy_bitcast_fusion), calls=%async_computation | async-start | bytes 2097152 | tf_op jit(solution)/shard_map/all_to_all | solution.py:58
  17.7 0.0 copy-start.2
  17.7 1.6 %copy.22 = bf16[128,4096]{0,1:T(8,128)(2,1)S(1)} copy(bf16[128,4096]{1,0:T(8,128)(2,1)} %param.5) | data formatting | bytes 2097152 | tf_op args[1]
  19.4 0.0 copy-start.1
  19.4 0.1 shift_right_arithmetic.23
  19.5 0.0 copy-done.2
  19.5 0.1 copy.23
  19.6 0.7 multiply_reduce_fusion
  20.3 25.7 %all-to-all-done = bf16[64,128,64]{1,2,0:T(8,128)(2,1)S(1)} async-done(((bf16[64,128,64]{1,2,0:T(8,128)(2,1)}), bf16[64,128,64]{1,2,0:T(8,128)(2,1)S(1)}, u32[]{:S(2)}, u32[]{:S(2)}) %all-to-all-start) | async-done | bytes 1048608 | tf_op jit(solution)/shard_map/all_to_all | solution.py:58
  46.0 0.0 copy-done.1
  46.0 2.0 %fusion.7 = (f32[4096]{0:T(1024)S(1)}, f32[128]{0:T(128)S(1)}) fusion(bf16[128,4096]{0,1:T(8,128)(2,1)S(1)} %copy.22, bf16[64,128,64]{1,2,0:T(8,128)(2,1)S(1)} %all-to-all-done, f32[128]{0:T(128)S(1)} %get-tuple-element.15, s32[4096]{0:T(1024)S(1)} %shift_right_arithmetic.23, s32[128,128]{0,1:T(8,128)S(1)} %copy.23, f32[4096]{0:T(1024)S(1)} %copy-done.1), kind=kLoop, calls=%fused_computation.9 | loop fusion | flops 6287232 | bytes 2212864 | tf_op jit(solution)/shard_map/reduce_sum | solution.py:50
  48.0 0.1 all_to_all.18
  48.1 15.5 %all_to_all.24 = f32[64,1,64]{2,1,0:T(1,128)S(1)} all-to-all(f32[64,1,64]{2,1,0:T(1,128)S(1)} %all_to_all.18), channel_id=1, replica_groups=mesh['aa'=12,'ba'=64] {'ba'}, dimensions={0} | all-to-all | bytes 32768 | tf_op jit(solution)/shard_map/all_to_all | solution.py:19
  63.7 0.6 broadcast_in_dim.2
  64.3 11.8 %all-to-all-start.2 = ((f32[12,1,64]{2,1,0:T(1,128)}), f32[12,1,64]{2,1,0:T(1,128)S(1)}, u32[]{:S(2)}, u32[]{:S(2)}) async-start(f32[12,1,64]{2,1,0:T(1,128)} %broadcast_in_dim.2), calls=%async_computation.2 | async-start | bytes 12288 | tf_op jit(solution)/shard_map/all_to_all | solution.py:25
  76.0 2.5 %fusion.6 = bf16[128,4096]{0,1:T(8,128)(2,1)} fusion(bf16[128,4096]{0,1:T(8,128)(2,1)S(1)} %copy.22, bf16[64,128,64]{1,2,0:T(8,128)(2,1)S(1)} %all-to-all-done, f32[128]{0:T(128)S(1)} %broadcast_multiply_fusion.2, f32[128]{0:T(128)S(1)} %get-tuple-element.15, f32[4096]{0:T(1024)S(1)} %copy-done.1, f32[128]{0:T(128)S(1)} %get-tuple-element.14, ...), kind=kLoop, calls=%fused_computation.8 | loop fusion | flops 7340032 | bytes 3245568 | tf_op jit(solution)/shard_map/convert_element_type | solution.py:49
  78.5 2.3 %copy.26 = bf16[128,4096]{1,0:T(8,128)(2,1)} copy(bf16[128,4096]{0,1:T(8,128)(2,1)} %fusion.6) | data formatting | bytes 2097152
  80.8 4.2 %all-to-all-done.2 = f32[12,1,64]{2,1,0:T(1,128)S(1)} async-done(((f32[12,1,64]{2,1,0:T(1,128)}), f32[12,1,64]{2,1,0:T(1,128)S(1)}, u32[]{:S(2)}, u32[]{:S(2)}) %all-to-all-start.2) | async-done | bytes 3104 | tf_op jit(solution)/shard_map/all_to_all | solution.py:25
  85.0 0.5 broadcast_multiply_fusion
  (5 shorter events, 0.1 us)
Async XLA Ops:
  0.6 1.2 %copy-start = (bf16[8192,64]{0,1:T(8,128)(2,1)S(1)}, bf16[8192,64]{0,1:T(8,128)(2,1)}, u32[]{:S(2)}) copy-start(bf16[8192,64]{0,1:T(8,128)(2,1)} %param.4) | copy-start | bytes 3145732
  3.1 42.9 %all-to-all-start = ((bf16[64,128,64]{1,2,0:T(8,128)(2,1)}), bf16[64,128,64]{1,2,0:T(8,128)(2,1)S(1)}, u32[]{:S(2)}, u32[]{:S(2)}) async-start(bf16[64,128,64]{1,2,0:T(8,128)(2,1)} %copy_bitcast_fusion), calls=%async_computation | async-start | bytes 2097152 | tf_op jit(solution)/shard_map/all_to_all | solution.py:58
  17.7 1.8 %copy-start.2 = (s32[128,128]{1,0:T(8,128)S(1)}, s32[128,128]{1,0:T(8,128)}, u32[]{:S(2)}) copy-start(s32[128,128]{1,0:T(8,128)} %param.6) | copy-start | bytes 196612
  19.4 26.6 %copy-start.1 = (f32[4096]{0:T(1024)S(1)}, f32[4096]{0:T(1024)}, u32[]{:S(2)}) copy-start(f32[4096]{0:T(1024)} %param.7) | copy-start | bytes 49156
  64.3 20.7 %all-to-all-start.2 = ((f32[12,1,64]{2,1,0:T(1,128)}), f32[12,1,64]{2,1,0:T(1,128)S(1)}, u32[]{:S(2)}, u32[]{:S(2)}) async-start(f32[12,1,64]{2,1,0:T(1,128)} %broadcast_in_dim.2), calls=%async_computation.2 | async-start | bytes 12288 | tf_op jit(solution)/shard_map/all_to_all | solution.py:25
where the time goes:
time: 85.9 us; the launch traced here: 85.5 us
  waiting for transfers between devices  29.9 us (35%)
  starting transfers between devices  26.3 us (31%)
  blocking collectives  15.5 us (18%)
  local copies, waits for them, and re-layouts  7.27 us (8%)
  other arithmetic  5.82 us (7%)
    all_to_all x1, waiting for transfers between devices, per_device(): lax.all_to_all(pieces, 'ba', split_axis=0, concat_axis=2, tiled=True)  25.7 us
    all_to_all x1, blocking collectives, sum_at_owner(): lax.all_to_all(parts, axis, split_axis=0, concat_axis=0, tiled=True)  15.5 us
    all_to_all x1, starting transfers between devices, per_device(): lax.all_to_all(pieces, 'ba', split_axis=0, concat_axis=2, tiled=True)  14.6 us
    all_to_all x1, starting transfers between devices, from_everyone(): lax.all_to_all(jnp.broadcast_to(value[None], (devices, *value.shape)), ax...  11.8 us
    unnamed x9, local copies, waits for them, and re-layouts  5.23 us
    all_to_all x1, waiting for transfers between devices, from_everyone(): lax.all_to_all(jnp.broadcast_to(value[None], (devices, *value.shape)), ax...  4.17 us
    convert_element_type x1, other arithmetic, rows_backward(): (inverse * (scaled - normed * centre) * keep * (1.0 / KEEP_RATE)).astype(...  2.48 us
    reduce_sum x1, other arithmetic, rows_backward(): partial_sum = jnp.sum(grads * normed, axis=0)  2.02 us
  transfers between devices with their start and end apart: 2, of which 2 were waited for; matrix products, arithmetic and copies ran while one was open for 9% of the time, Pallas kernels for 0%

commit v1 on v0

--- a/solution.py
+++ b/solution.py
@@ -7,29 +7,30 @@
 
 KEEP_RATE = 0.9
 EPSILON = 1e-06
+FIRST_BA = 36
+FIRST_AA = 9
 
 
-def split_up(value, dim, devices):
-    before, after = (value.shape[:dim], value.shape[dim + 1 :])
-    return jnp.moveaxis(value.reshape(*before, devices, -1, *after), dim, 0)
+def rotated(devices, first):
+    return [[(first + i) % devices for i in range(devices)]]
 
 
-def sum_at_owner(value, axis, dim):
-    parts = split_up(value, dim, lax.axis_size(axis))
-    arrived = lax.all_to_all(parts, axis, split_axis=0, concat_axis=0, tiled=True)
-    return arrived.sum(axis=0)
+def roll(value, shift):
+    return jnp.concatenate([value[shift:], value[:shift]], axis=0)
 
 
-def from_everyone(value, axis):
+def exchange(parts, axis, first):
     devices = lax.axis_size(axis)
-    return lax.all_to_all(
-        jnp.broadcast_to(value[None], (devices, *value.shape)), axis, 0, 0, tiled=True
+    arrived = lax.all_to_all(
+        roll(parts, first), axis, 0, 0, tiled=True, axis_index_groups=rotated(devices, first)
     )
+    return roll(arrived, devices - first)
 
 
-def over_copies(value, axis):
-    everything = from_everyone(value, axis)
-    return jnp.sum(everything, axis=0)
+def sum_over(parts, axis, first):
+    devices = lax.axis_size(axis)
+    arrived = lax.all_to_all(parts, axis, 0, 0, tiled=True, axis_index_groups=rotated(devices, first))
+    return jnp.sum(arrived, axis=0)
 
 
 def unpack_bits(words):
@@ -55,12 +56,13 @@
     groups = lax.axis_size("ba")
     rows = grad_out.shape[0] // groups
     pieces = grad_out.reshape(groups, rows, grad_out.shape[1])
-    arrived = lax.all_to_all(pieces, "ba", split_axis=0, concat_axis=2, tiled=True)
-    grad_rows = arrived.reshape(rows, arrived.shape[2])
+    arrived = exchange(pieces, "ba", FIRST_BA)
+    grad_rows = jnp.moveaxis(arrived, 0, 1).reshape(rows, -1)
     grad_in, partial_sum = rows_backward(grad_rows, saved_input, keep_bits, gain)
     total_tokens = rows * groups * lax.axis_size("aa")
-    owned = sum_at_owner(partial_sum, "ba", 0)
-    share = over_copies(owned, "aa")
+    owned = sum_over(roll(partial_sum.reshape(groups, -1), FIRST_BA), "ba", FIRST_BA)
+    copies = jnp.broadcast_to(owned[None], (lax.axis_size("aa"), *owned.shape))
+    share = sum_over(copies, "aa", FIRST_AA)
     gain_grad = share * (1.0 / math.sqrt(total_tokens))
     return (grad_in, gain_grad)
 

time: 85.9 us -> 79.7 us (0.928)
  waiting for transfers between devices: 29.9 us -> 23.3 us
  starting transfers between devices: 26.3 us -> 29.6 us
  blocking collectives: 15.5 us -> 12.6 us
    all_to_all x2, waiting for transfers between devices: 29.9 us -> 23.3 us  [the longest x1 20.9 us: exchange(): lax.all_to_all(roll(parts, first), axis, 0, 0, tiled=True, axis_index_gro...]
    all_to_all x2, starting transfers between devices: 26.3 us -> 29.6 us  [the longest x1 20.5 us: exchange(): lax.all_to_all(roll(parts, first), axis, 0, 0, tiled=True, axis_index_gro...]
    all_to_all x1, blocking collectives: 15.5 us -> 12.6 us  [sum_over(): lax.all_to_all(parts, axis, 0, 0, tiled=True, axis_index_groups=rotated(d...]
    unnamed x9 -> x7, local copies, waits for them, and re-layouts: 5.23 us -> 3.03 us
    slice x0 -> x12, local copies, waits for them, and re-layouts: none -> 1.82 us  [roll(): return jnp.concatenate([value[shift:], value[:shift]], axis=0)]
    concatenate x0 -> x1, local copies, waits for them, and re-layouts: none -> 1.65 us  [roll(): return jnp.concatenate([value[shift:], value[:shift]], axis=0)]
    reshape x1 -> x0, local copies, waits for them, and re-layouts: 1.27 us -> none  [per_device(): pieces = grad_out.reshape(groups, rows, grad_out.shape[1])]
    convert_element_type x1, other arithmetic: 2.48 us -> 1.62 us  [rows_backward(): (inverse * (scaled - normed * centre) * keep * (1.0 / KEEP_RATE)).astype(...]
  transfers between devices with their start and end apart: 2 -> 2, of which waited for: 2 -> 2; matrix products, arithmetic and copies ran while one was open for 9% -> 7% of each run, Pallas kernels for 0% -> 0%
where the time goes in v1:
time: 79.7 us; the launch traced here: 78.8 us
  starting transfers between devices  29.6 us (37%)
  waiting for transfers between devices  23.3 us (29%)
  blocking collectives  12.6 us (16%)
  local copies, waits for them, and re-layouts  7.18 us (9%)
  other arithmetic  5.36 us (7%)
    all_to_all x1, waiting for transfers between devices, exchange(): lax.all_to_all(roll(parts, first), axis, 0, 0, tiled=True, axis_index_gro...  20.9 us
    all_to_all x1, starting transfers between devices, exchange(): lax.all_to_all(roll(parts, first), axis, 0, 0, tiled=True, axis_index_gro...  20.5 us
    all_to_all x1, blocking collectives, sum_over(): lax.all_to_all(parts, axis, 0, 0, tiled=True, axis_index_groups=rotated(d...  12.6 us
    all_to_all x1, starting transfers between devices, sum_over(): lax.all_to_all(parts, axis, 0, 0, tiled=True, axis_index_groups=rotated(d...  9.09 us
    unnamed x7, local copies, waits for them, and re-layouts  3.03 us
    all_to_all x1, waiting for transfers between devices, sum_over(): lax.all_to_all(parts, axis, 0, 0, tiled=True, axis_index_groups=rotated(d...  2.45 us
    reduce_sum x1, other arithmetic, rows_backward(): partial_sum = jnp.sum(grads * normed, axis=0)  2.02 us
    slice x12, local copies, waits for them, and re-layouts, roll(): return jnp.concatenate([value[shift:], value[:shift]], axis=0)  1.82 us
  transfers between devices with their start and end apart: 2, of which 2 were waited for; matrix products, arithmetic and copies ran while one was open for 7% of the time, Pallas kernels for 0%

profile of v1, /device:TPU:1, one launch (start us, length us, event | category | flops | bytes accessed | tf_op | source)
XLA Modules:
  0.0 78.8 jit_solution(16728064589545698202)
XLA Ops:
  0.6 0.0 slice-start
  0.6 0.0 slice-start.1
  0.6 1.0 %slice-done = bf16[3584,64]{0,1:T(8,128)(2,1)S(1)} async-done(((bf16[8192,64]{0,1:T(8,128)(2,1)}), bf16[3584,64]{0,1:T(8,128)(2,1)S(1)}, s32[]{:S(2)}) %slice-start) | async-done | bytes 458776 | tf_op jit(solution)/shard_map/slice | solution.py:19
  1.6 0.3 slice.47
  1.9 0.0 slice-done.1
  1.9 0.3 slice.49
  2.3 0.3 pad_maximum_fusion
  2.6 1.6 %copy.18 = bf16[64,128,64]{1,2,0:T(8,128)(2,1)} copy(bf16[64,128,64]{1,0,2:T(8,128)(2,1)S(1)} %pad_maximum_fusion) | data formatting | bytes 2097152 | tf_op jit(solution)/shard_map/concatenate | solution.py:19
  4.3 0.0 copy-start.1
  4.3 20.5 %all-to-all-start = ((bf16[64,128,64]{1,2,0:T(8,128)(2,1)}), bf16[64,128,64]{1,2,0:T(8,128)(2,1)S(1)}, u32[]{:S(2)}, u32[]{:S(2)}) async-start(bf16[64,128,64]{1,2,0:T(8,128)(2,1)} %copy.18), calls=%async_computation | async-start | bytes 2097152 | tf_op jit(solution)/shard_map/all_to_all | solution.py:24
  24.7 0.0 copy-done.1
  24.7 0.1 copy.17
  24.8 0.1 shift_right_arithmetic.23
  24.9 1.6 %copy.16 = bf16[128,4096]{0,1:T(8,128)(2,1)S(1)} copy(bf16[128,4096]{1,0:T(8,128)(2,1)} %param.5) | data formatting | bytes 2097152 | tf_op args[1]
  26.6 0.7 multiply_reduce_fusion
  27.3 0.0 copy-start
  27.3 20.9 %all-to-all-done = bf16[64,128,64]{1,2,0:T(8,128)(2,1)S(1)} async-done(((bf16[64,128,64]{1,2,0:T(8,128)(2,1)}), bf16[64,128,64]{1,2,0:T(8,128)(2,1)S(1)}, u32[]{:S(2)}, u32[]{:S(2)}) %all-to-all-start) | async-done | bytes 1048608 | tf_op jit(solution)/shard_map/all_to_all | solution.py:24
  48.2 0.0 copy-done
  48.2 2.0 %fusion.7 = (f32[4096]{0:T(1024)S(1)}, f32[128]{0:T(128)S(1)}) fusion(bf16[128,4096]{0,1:T(8,128)(2,1)S(1)} %copy.16, f32[128]{0:T(128)S(1)} %get-tuple-element.11, s32[4096]{0:T(1024)S(1)} %shift_right_arithmetic.23, s32[128,128]{0,1:T(8,128)S(1)} %copy.17, bf16[28,128,64]{1,2,0:T(8,128)(2,1)S(1)} %slice.57, bf16[36,128,64]{1,2,0:T(8,128)(2,1)S(1)} %slice.56, ...), kind=kLoop, calls=%fused_computation.9 | loop fusion | flops 7860096 | bytes 2212864 | tf_op jit(solution)/shard_map/reduce_sum | solution.py:51
  50.3 0.1 slice.55
  50.4 0.1 slice.53
  50.5 12.6 %all_to_all.20 = f32[64,1,64]{2,1,0:T(1,128)S(1)} all-to-all(f32[64,1,64]{2,1,0:T(1,128)S(1)} %bitcast.46), channel_id=1, replica_groups={{36,37,38,39,40,41,42,43,44,45,46,47,48,49,50,51,52,53,54,55,56,57,58,5..., dimensions={0} | all-to-all | bytes 32768 | tf_op jit(solution)/shard_map/all_to_all | solution.py:32
  63.1 0.1 reduce_sum.48
  63.2 0.6 broadcast_in_dim.2
  63.8 9.1 %all-to-all-start.2 = ((f32[12,1,64]{2,1,0:T(1,128)}), f32[12,1,64]{2,1,0:T(1,128)S(1)}, u32[]{:S(2)}, u32[]{:S(2)}) async-start(f32[12,1,64]{2,1,0:T(1,128)} %broadcast_in_dim.2), calls=%async_computation.2 | async-start | bytes 12288 | tf_op jit(solution)/shard_map/all_to_all | solution.py:32
  72.9 1.6 %fusion.6 = bf16[128,4096]{0,1:T(8,128)(2,1)S(1)} fusion(bf16[128,4096]{0,1:T(8,128)(2,1)S(1)} %copy.16, f32[128]{0:T(128)S(1)} %broadcast_multiply_fusion.2, f32[128]{0:T(128)S(1)} %get-tuple-element.11, f32[4096]{0:T(1024)S(1)} %copy-done, f32[128]{0:T(128)S(1)} %get-tuple-element.10, s32[4096]{0:T(1024)S(1)} %shift_right_arithmetic.23, ...), kind=kLoop, calls=%fused_computation.8 | loop fusion | flops 8912896 | bytes 3245568 | tf_op jit(solution)/shard_map/convert_element_type | solution.py:50
  74.5 1.3 %copy.19 = bf16[128,4096]{1,0:T(8,128)(2,1)} copy(bf16[128,4096]{0,1:T(8,128)(2,1)S(1)} %fusion.6) | data formatting | bytes 2097152
  75.8 2.4 %all-to-all-done.2 = f32[12,1,64]{2,1,0:T(1,128)S(1)} async-done(((f32[12,1,64]{2,1,0:T(1,128)}), f32[12,1,64]{2,1,0:T(1,128)S(1)}, u32[]{:S(2)}, u32[]{:S(2)}) %all-to-all-start.2) | async-done | bytes 3104 | tf_op jit(solution)/shard_map/all_to_all | solution.py:32
  78.3 0.5 broadcast_multiply_fusion
  (9 shorter events, 0.1 us)
Async XLA Ops:
  0.6 1.0 %slice-start = ((bf16[8192,64]{0,1:T(8,128)(2,1)}), bf16[3584,64]{0,1:T(8,128)(2,1)S(1)}, s32[]{:S(2)}) async-start(bf16[8192,64]{0,1:T(8,128)(2,1)} %param.4), calls=%async_computation.3 | async-start | bytes 917504 | tf_op jit(solution)/shard_map/slice | solution.py:19
  0.6 1.3 %slice-start.1 = ((bf16[8192,64]{0,1:T(8,128)(2,1)}), bf16[4608,64]{0,1:T(8,128)(2,1)S(1)}, s32[]{:S(2)}) async-start(bf16[8192,64]{0,1:T(8,128)(2,1)} %param.4), calls=%async_computation.4 | async-start | bytes 1179648 | tf_op jit(solution)/shard_map/slice | solution.py:19
  4.3 20.5 %copy-start.1 = (s32[128,128]{1,0:T(8,128)S(1)}, s32[128,128]{1,0:T(8,128)}, u32[]{:S(2)}) copy-start(s32[128,128]{1,0:T(8,128)} %param.6) | copy-start | bytes 196612
  4.3 43.9 %all-to-all-start = ((bf16[64,128,64]{1,2,0:T(8,128)(2,1)}), bf16[64,128,64]{1,2,0:T(8,128)(2,1)S(1)}, u32[]{:S(2)}, u32[]{:S(2)}) async-start(bf16[64,128,64]{1,2,0:T(8,128)(2,1)} %copy.18), calls=%async_computation | async-start | bytes 2097152 | tf_op jit(solution)/shard_map/all_to_all | solution.py:24
  27.3 20.9 %copy-start = (f32[4096]{0:T(1024)S(1)}, f32[4096]{0:T(1024)}, u32[]{:S(2)}) copy-start(f32[4096]{0:T(1024)} %param.7) | copy-start | bytes 49156
  63.8 14.5 %all-to-all-start.2 = ((f32[12,1,64]{2,1,0:T(1,128)}), f32[12,1,64]{2,1,0:T(1,128)S(1)}, u32[]{:S(2)}, u32[]{:S(2)}) async-start(f32[12,1,64]{2,1,0:T(1,128)} %broadcast_in_dim.2), calls=%async_computation.2 | async-start | bytes 12288 | tf_op jit(solution)/shard_map/all_to_all | solution.py:32

commit v2 on v1

v2 whole, which is shorter than its diff:
```python
import functools
import math

import jax
import jax.numpy as jnp
from jax import lax
from jax.experimental import pallas as pl
from jax.experimental.pallas import tpu as pltpu
from jax.sharding import PartitionSpec as P

KEEP_RATE = 0.9
EPSILON = 1e-06
LANES = 128
BITS = 32
CHUNKS = 4
FIRST_BA = 36
FIRST_AA = 9
F32 = jnp.float32


def rotation(devices, first):
    return [(first + i) % devices for i in range(devices)]


def exchange(parts, axis, order):
    return lax.all_to_all(parts, axis, 0, 0, tiled=True, axis_index_groups=[order])


def params(mib):
    return pltpu.CompilerParams(vmem_limit_bytes=mib << 20)


def cost(flops, size):
    return pl.CostEstimate(flops=flops, bytes_accessed=size, transcendentals=0)


def arrange_kernel(order, grads, out, held, arrive, leave):
    devices, _, rows = out.shape
    each = devices // CHUNKS
    place = {device: i for i, device in enumerate(order)}

    def chunk(k):
        part = pl.ds(k * each * rows, each * rows)
        return pltpu.make_async_copy(grads.at[:, part], held.at[:, part], arrive.at[k])

    for k in range(CHUNKS):
        chunk(k).start()
    for k in range(CHUNKS):
        chunk(k).wait()
        for d in range(k * each, (k + 1) * each):
            piece = held.at[:, pl.ds(d * rows, rows)]
            pltpu.make_async_copy(piece, out.at[place[d]], leave).start()
    pltpu.make_async_copy(out, out, leave).wait()


def arrange(grads, order):
    features, tokens = grads.shape
    devices = len(order)
    return pl.pallas_call(
        functools.partial(arrange_kernel, order),
        out_shape=jax.ShapeDtypeStruct((devices, features, tokens // devices), grads.dtype),
        in_specs=[pl.BlockSpec(memory_space=pl.ANY)],
        out_specs=pl.BlockSpec(memory_space=pl.ANY),
        scratch_shapes=[
            pltpu.VMEM(grads.shape, grads.dtype),
            pltpu.SemaphoreType.DMA((CHUNKS,)),
            pltpu.SemaphoreType.DMA,
        ],
        cost_estimate=cost(10**6, 4 * grads.size),
        name="arrange",
    )(grads)


def keep_flags(words_t, q, rows):
    count = LANES // BITS
    shift = lax.broadcasted_iota(jnp.int32, (count, BITS, rows), 1)
    word = jnp.broadcast_to(words_t[q * count : (q + 1) * count, None, :], (count, BITS, rows))
    return (jnp.right_shift(word, shift) & 1).reshape(LANES, rows).astype(F32)


def unpack_kernel(order, inputs, words, by_device, scale):
    rows, width = inputs.shape
    features = width // len(order)
    words_t = words[...].T
    squares = jnp.zeros((8, rows), F32)
    place = {device: i for i, device in enumerate(order)}
    for q in range(width // LANES):
        at = slice(q * LANES, (q + 1) * LANES)
        value = inputs[:, at].astype(F32).T * keep_flags(words_t, q, rows)
        dropped = value * (1.0 / KEEP_RATE)
        squares += jnp.sum((dropped * dropped).reshape(LANES // 8, 8, rows), axis=0)
        for h in range(LANES // features):
            piece = value[h * features : (h + 1) * features, :]
            by_device[place[q * LANES // features + h]] = piece.astype(by_device.dtype)
    mean = jnp.sum(squares, axis=0, keepdims=True) * (1.0 / width)
    scale[...] = lax.rsqrt(mean + EPSILON) * (1.0 / KEEP_RATE)


def unpack(inputs, words, order):
    rows, width = inputs.shape
    devices = len(order)
    return pl.pallas_call(
        functools.partial(unpack_kernel, order),
        out_shape=(
            jax.ShapeDtypeStruct((devices, width // devices, rows), inputs.dtype),
            jax.ShapeDtypeStruct((1, rows), F32),
        ),
        compiler_params=params(6),
        cost_estimate=cost(10**8, 4 * inputs.size),
        name="unpack",
    )(inputs, words)


def token_sums_kernel(grads, inputs, scale, out):
    devices, features, rows = grads.shape
    shape = (features, LANES)
    diagonal = lax.broadcasted_iota(jnp.int32, shape, 0) == lax.broadcasted_iota(jnp.int32, shape, 1)
    for d in range(devices):
        product = grads[d].astype(F32) * (inputs[d].astype(F32) * scale[...])
        sums = jnp.sum(product, axis=1, keepdims=True)
        out[d : d + 1, :] = jnp.sum(jnp.where(diagonal, sums, 0.0), axis=0, keepdims=True)


def token_sums(grads, inputs, scale):
    return pl.pallas_call(
        token_sums_kernel,
        out_shape=jax.ShapeDtypeStruct((grads.shape[0], LANES), F32),
        compiler_params=params(6),
        cost_estimate=cost(10**7, 4 * grads.size),
        name="token_sums",
    )(grads, inputs, scale)


def input_grad_kernel(order, grads, inputs, words, scale, gain, out, scaled, normed, factor):
    rows, width = out.shape
    features = width // len(order)
    place = {device: i for i, device in enumerate(order)}
    words_t = words[...].T
    column = jnp.broadcast_to(scale[...], (LANES, rows)).T
    total = jnp.zeros((rows, LANES), F32)
    for q in range(width // LANES):
        at = slice(q * LANES, (q + 1) * LANES)
        parts = [grads[place[q * LANES // features + h]] for h in range(LANES // features)]
        value = jnp.concatenate(parts, axis=0).astype(F32).T * gain[:, at]
        kept = keep_flags(words_t, q, rows).T * column
        norm = inputs[:, at].astype(F32) * kept
        scaled[:, at] = value
        normed[:, at] = norm
        factor[:, at] = kept
        total += value * norm
    centre = jnp.sum(total, axis=1, keepdims=True) * (1.0 / width)
    for q in range(width // LANES):
        at = slice(q * LANES, (q + 1) * LANES)
        value = factor[:, at] * (scaled[:, at] - normed[:, at] * centre)
        out[:, at] = value.astype(out.dtype)


def input_grad(grads, inputs, words, scale, gain, order):
    rows, width = inputs.shape
    return pl.pallas_call(
        functools.partial(input_grad_kernel, order),
        out_shape=jax.ShapeDtypeStruct((rows, width), inputs.dtype),
        scratch_shapes=[pltpu.VMEM((rows, width), F32)] * 3,
        compiler_params=params(14),
        cost_estimate=cost(10**8, 8 * inputs.size),
        name="input_grad",
    )(grads, inputs, words, scale, gain.reshape(1, width))


def per_device(grad_out, saved_input, keep_bits, gain):
    groups, planes = lax.axis_size("ba"), lax.axis_size("aa")
    features = grad_out.shape[1]
    rows = saved_input.shape[0]
    order, order_aa = rotation(groups, FIRST_BA), rotation(planes, FIRST_AA)

    arrived = exchange(arrange(grad_out.T, order), "ba", order)
    by_device, scale = unpack(saved_input, keep_bits, order)
    partial_sum = token_sums(arrived, by_device, scale)
    owned = jnp.sum(exchange(partial_sum[:, None, :], "ba", order), axis=0)
    copies = jnp.broadcast_to(owned[None], (planes, *owned.shape))
    share = jnp.sum(exchange(copies, "aa", order_aa), axis=0).reshape(-1)[:features]
    gain_grad = share * (1.0 / math.sqrt(rows * groups * planes))

    late, _ = lax.optimization_barrier((arrived, owned))
    grad_in = input_grad(late, saved_input, keep_bits, scale, gain, order)
    return (grad_in, gain_grad)


def solution(mesh):
    placed = (P("aa", "ba"), P(("aa", "ba"), None), P(("aa", "ba"), None), P())
    return jax.shard_map(
        per_device,
        mesh=mesh,
        in_specs=placed,
        out_specs=(P(("aa", "ba"), None), P("ba")),
        check_vma=False,
    )
```

time: 79.7 us -> 76.4 us (0.959)
  local copies, waits for them, and re-layouts: 7.18 us -> 0.61 us
  Pallas kernels: 0 us -> 5.83 us
  other arithmetic: 5.36 us -> 0.63 us
  waiting for transfers between devices: 23.3 us -> 25.5 us
    pallas_call x0 -> x4, Pallas kernels: none -> 5.83 us  [the longest x1 2.44 us: input_grad(): pl.pallas_call(functools.partial(input_grad_kernel, order), out_shape=jax...]
    unnamed x7 -> x6, local copies, waits for them, and re-layouts: 3.03 us -> 0.02 us
    reduce_sum x4 -> x2, other arithmetic: 2.86 us -> 0.11 us  [the longest x1 0.08 us: per_device(): owned = jnp.sum(exchange(partial_sum[:, None, :], 'ba', order), axis=0)]
    all_to_all x2, waiting for transfers between devices: 23.3 us -> 25.5 us  [exchange(): lax.all_to_all(parts, axis, 0, 0, tiled=True, axis_index_groups=[order])]
    slice x12 -> x0, local copies, waits for them, and re-layouts: 1.82 us -> none  [roll(): return jnp.concatenate([value[shift:], value[:shift]], axis=0)]
    concatenate x1 -> x0, local copies, waits for them, and re-layouts: 1.65 us -> none  [roll(): return jnp.concatenate([value[shift:], value[:shift]], axis=0)]
    convert_element_type x1 -> x0, other arithmetic: 1.62 us -> none  [rows_backward(): (inverse * (scaled - normed * centre) * keep * (1.0 / KEEP_RATE)).astype(...]
  transfers between devices with their start and end apart: 2 -> 2, of which waited for: 2 -> 2; matrix products, arithmetic and copies ran while one was open for 7% -> 0% of each run, Pallas kernels for 0% -> 4%
where the time goes in v2:
time: 76.4 us; the launch traced here: 75.5 us
  starting transfers between devices  29.6 us (39%)
  waiting for transfers between devices  25.5 us (33%)
  blocking collectives  12.6 us (16%)
  Pallas kernels  5.83 us (8%)
    all_to_all x2, starting transfers between devices, exchange(): lax.all_to_all(parts, axis, 0, 0, tiled=True, axis_index_groups=[order])  29.6 us
    all_to_all x2, waiting for transfers between devices, exchange(): lax.all_to_all(parts, axis, 0, 0, tiled=True, axis_index_groups=[order])  25.5 us
    all_to_all x1, blocking collectives, exchange(): lax.all_to_all(parts, axis, 0, 0, tiled=True, axis_index_groups=[order])  12.6 us
    pallas_call x1, Pallas kernels, input_grad(): pl.pallas_call(functools.partial(input_grad_kernel, order), out_shape=jax...  2.44 us
    pallas_call x1, Pallas kernels, arrange(): pl.pallas_call(functools.partial(arrange_kernel, order), out_shape=jax.Sh...  1.93 us
  transfers between devices with their start and end apart: 2, of which 2 were waited for; matrix products, arithmetic and copies ran while one was open for 0% of the time, Pallas kernels for 4%

profile of v2, /device:TPU:1, one launch (start us, length us, event | category | flops | bytes accessed | tf_op | source)
XLA Modules:
  0.0 75.5 jit_solution(6060798396155354508)
XLA Ops:
  0.6 1.9 %arrange.1 = bf16[64,64,128]{2,1,0:T(8,128)(2,1)} custom-call(bf16[64,8192]{1,0:T(8,128)(2,1)} %bitcast.10), custom_call_target="tpu_custom_call" | custom-call | flops 1000000 | bytes 2097152 | tf_op jit(solution)/shard_map/arrange/pallas_call | solution.py:59
  2.6 0.0 copy-start
  2.6 0.0 copy-start.1
  2.6 20.5 %all-to-all-start = ((bf16[64,64,128]{2,1,0:T(8,128)(2,1)}), bf16[64,64,128]{2,1,0:T(8,128)(2,1)S(1)}, u32[]{:S(2)}, u32[]{:S(2)}) async-start(bf16[64,64,128]{2,1,0:T(8,128)(2,1)} %arrange.1), calls=%async_computation | async-start | bytes 2097152 | tf_op jit(solution)/shard_map/all_to_all | solution.py:26
  23.1 0.0 copy-done
  23.1 0.0 copy-done.1
  23.1 0.8 %unpack.1 = (bf16[64,64,128]{2,1,0:T(8,128)(2,1)S(1)}, f32[1,128]{1,0:T(1,128)S(1)}) custom-call(bf16[128,4096]{1,0:T(8,128)(2,1)S(1)} %copy-done, s32[128,128]{1,0:T(8,128)S(1)} %copy-done.1), custom_call_target="tpu_custom_call" | custom-call | flops 100000000 | bytes 2097152 | tf_op jit(solution)/shard_map/unpack/pallas_call | solution.py:102
  23.9 22.6 %all-to-all-done.grads = bf16[64,64,128]{2,1,0:T(8,128)(2,1)S(1)} async-done(((bf16[64,64,128]{2,1,0:T(8,128)(2,1)}), bf16[64,64,128]{2,1,0:T(8,128)(2,1)S(1)}, u32[]{:S(2)}, u32[]{:S(2)}) %all-to-all-start) | async-done | bytes 1048608 | tf_op jit(solution)/shard_map/all_to_all | solution.py:26
  46.5 0.6 token_sums.1
  47.1 12.6 %all_to_all.15 = f32[64,1,128]{2,1,0:T(1,128)S(1)} all-to-all(f32[64,1,128]{2,1,0:T(1,128)S(1)} %bitcast.8), channel_id=1, replica_groups={{36,37,38,39,40,41,42,43,44,45,46,47,48,49,50,51,52,53,54,55,56,57,58,5..., dimensions={0} | all-to-all | bytes 65536 | tf_op jit(solution)/shard_map/all_to_all | solution.py:26
  59.8 0.1 reduce_sum.20
  59.8 0.0 copy-start.2
  59.8 0.6 broadcast_in_dim.10
  60.4 9.1 %all-to-all-start.2 = ((f32[12,1,128]{2,1,0:T(1,128)}), f32[12,1,128]{2,1,0:T(1,128)S(1)}, u32[]{:S(2)}, u32[]{:S(2)}) async-start(f32[12,1,128]{2,1,0:T(1,128)} %broadcast_in_dim.10), calls=%async_computation.2 | async-start | bytes 12288 | tf_op jit(solution)/shard_map/all_to_all | solution.py:26
  69.5 0.0 copy-done.2
  69.5 2.4 %input_grad.1 = bf16[128,4096]{1,0:T(8,128)(2,1)} custom-call(bf16[64,64,128]{2,1,0:T(8,128)(2,1)S(1)} %all-to-all-done.grads, bf16[128,4096]{1,0:T(8,128)(2,1)S(1)} %copy-done, s32[128,128]{1,0:T(8,128)S(1)} %copy-done.1, f32[1,128]{1,0:T(1,128)S(1)} %get-tuple-element.4.scale, f32[1,4096]{1,0:T(1,128)S(1)} %bitcast.9), custom_call_target="tpu_custom_call" | custom-call | flops 100000000 | bytes 4194304 | tf_op jit(solution)/shard_map/input_grad/pallas_call | solution.py:160
  72.0 2.9 %all-to-all-done.2 = f32[12,1,128]{2,1,0:T(1,128)S(1)} async-done(((f32[12,1,128]{2,1,0:T(1,128)}), f32[12,1,128]{2,1,0:T(1,128)S(1)}, u32[]{:S(2)}, u32[]{:S(2)}) %all-to-all-start.2) | async-done | bytes 6176 | tf_op jit(solution)/shard_map/all_to_all | solution.py:26
  74.9 0.5 multiply_bitcast_fusion
  (1 shorter events, 0.0 us)
Async XLA Ops:
  2.6 20.5 %copy-start = (bf16[128,4096]{1,0:T(8,128)(2,1)S(1)}, bf16[128,4096]{1,0:T(8,128)(2,1)}, u32[]{:S(2)}) copy-start(bf16[128,4096]{1,0:T(8,128)(2,1)} %inputs.3) | copy-start | bytes 3145732
  2.6 20.5 %copy-start.1 = (s32[128,128]{1,0:T(8,128)S(1)}, s32[128,128]{1,0:T(8,128)}, u32[]{:S(2)}) copy-start(s32[128,128]{1,0:T(8,128)} %words.3) | copy-start | bytes 196612
  2.6 43.9 %all-to-all-start = ((bf16[64,64,128]{2,1,0:T(8,128)(2,1)}), bf16[64,64,128]{2,1,0:T(8,128)(2,1)S(1)}, u32[]{:S(2)}, u32[]{:S(2)}) async-start(bf16[64,64,128]{2,1,0:T(8,128)(2,1)} %arrange.1), calls=%async_computation | async-start | bytes 2097152 | tf_op jit(solution)/shard_map/all_to_all | solution.py:26
  59.8 9.7 %copy-start.2 = (f32[4096]{0:T(1024)S(1)}, f32[4096]{0:T(1024)}, u32[]{:S(2)}) copy-start(f32[4096]{0:T(1024)} %param.7) | copy-start | bytes 49156
  60.4 14.5 %all-to-all-start.2 = ((f32[12,1,128]{2,1,0:T(1,128)}), f32[12,1,128]{2,1,0:T(1,128)S(1)}, u32[]{:S(2)}, u32[]{:S(2)}) async-start(f32[12,1,128]{2,1,0:T(1,128)} %broadcast_in_dim.10), calls=%async_computation.2 | async-start | bytes 12288 | tf_op jit(solution)/shard_map/all_to_all | solution.py:26

commit v3 on v2

--- a/solution.py
+++ b/solution.py
@@ -12,8 +12,7 @@
 EPSILON = 1e-06
 LANES = 128
 BITS = 32
-CHUNKS = 4
-FIRST_BA = 36
+FIRST_BA = 37
 FIRST_AA = 9
 F32 = jnp.float32
 
@@ -34,43 +33,6 @@
     return pl.CostEstimate(flops=flops, bytes_accessed=size, transcendentals=0)
 
 
-def arrange_kernel(order, grads, out, held, arrive, leave):
-    devices, _, rows = out.shape
-    each = devices // CHUNKS
-    place = {device: i for i, device in enumerate(order)}
-
-    def chunk(k):
-        part = pl.ds(k * each * rows, each * rows)
-        return pltpu.make_async_copy(grads.at[:, part], held.at[:, part], arrive.at[k])
-
-    for k in range(CHUNKS):
-        chunk(k).start()
-    for k in range(CHUNKS):
-        chunk(k).wait()
-        for d in range(k * each, (k + 1) * each):
-            piece = held.at[:, pl.ds(d * rows, rows)]
-            pltpu.make_async_copy(piece, out.at[place[d]], leave).start()
-    pltpu.make_async_copy(out, out, leave).wait()
-
-
-def arrange(grads, order):
-    features, tokens = grads.shape
-    devices = len(order)
-    return pl.pallas_call(
-        functools.partial(arrange_kernel, order),
-        out_shape=jax.ShapeDtypeStruct((devices, features, tokens // devices), grads.dtype),
-        in_specs=[pl.BlockSpec(memory_space=pl.ANY)],
-        out_specs=pl.BlockSpec(memory_space=pl.ANY),
-        scratch_shapes=[
-            pltpu.VMEM(grads.shape, grads.dtype),
-            pltpu.SemaphoreType.DMA((CHUNKS,)),
-            pltpu.SemaphoreType.DMA,
-        ],
-        cost_estimate=cost(10**6, 4 * grads.size),
-        name="arrange",
-    )(grads)
-
-
 def keep_flags(words_t, q, rows):
     count = LANES // BITS
     shift = lax.broadcasted_iota(jnp.int32, (count, BITS, rows), 1)
@@ -78,37 +40,61 @@
     return (jnp.right_shift(word, shift) & 1).reshape(LANES, rows).astype(F32)
 
 
-def unpack_kernel(order, inputs, words, by_device, scale):
+def prepare_kernel(
+    order, grads, inputs, words, pieces, by_device, scale, rows_in, words_in, kept, rows_sem, words_sem, move
+):
     rows, width = inputs.shape
     features = width // len(order)
-    words_t = words[...].T
-    squares = jnp.zeros((8, rows), F32)
     place = {device: i for i, device in enumerate(order)}
+    words_copy = pltpu.make_async_copy(words, words_in, words_sem)
+    rows_copy = pltpu.make_async_copy(inputs, rows_in, rows_sem)
+    words_copy.start()
+    rows_copy.start()
+    for i, device in enumerate(order):
+        pltpu.make_async_copy(grads.at[:, pl.ds(device * rows, rows)], pieces.at[i], move).start()
+    words_copy.wait()
+    words_t = words_in[...].T
     for q in range(width // LANES):
         at = slice(q * LANES, (q + 1) * LANES)
-        value = inputs[:, at].astype(F32).T * keep_flags(words_t, q, rows)
-        dropped = value * (1.0 / KEEP_RATE)
+        kept[at, :] = keep_flags(words_t, q, rows).astype(kept.dtype)
+    rows_copy.wait()
+    squares = jnp.zeros((8, rows), F32)
+    for q in range(width // LANES):
+        at = slice(q * LANES, (q + 1) * LANES)
+        value = rows_in[:, at].T * kept[at, :]
+        dropped = value.astype(F32) * (1.0 / KEEP_RATE)
         squares += jnp.sum((dropped * dropped).reshape(LANES // 8, 8, rows), axis=0)
         for h in range(LANES // features):
-            piece = value[h * features : (h + 1) * features, :]
-            by_device[place[q * LANES // features + h]] = piece.astype(by_device.dtype)
+            by_device[place[q * LANES // features + h]] = value[h * features : (h + 1) * features, :]
     mean = jnp.sum(squares, axis=0, keepdims=True) * (1.0 / width)
     scale[...] = lax.rsqrt(mean + EPSILON) * (1.0 / KEEP_RATE)
+    pltpu.make_async_copy(pieces, pieces, move).wait()
 
 
-def unpack(inputs, words, order):
+def prepare(grads, inputs, words, order):
     rows, width = inputs.shape
     devices = len(order)
+    shape = (devices, width // devices, rows)
     return pl.pallas_call(
-        functools.partial(unpack_kernel, order),
+        functools.partial(prepare_kernel, order),
         out_shape=(
-            jax.ShapeDtypeStruct((devices, width // devices, rows), inputs.dtype),
+            jax.ShapeDtypeStruct(shape, grads.dtype),
+            jax.ShapeDtypeStruct(shape, inputs.dtype),
             jax.ShapeDtypeStruct((1, rows), F32),
         ),
+        in_specs=[pl.BlockSpec(memory_space=pltpu.HBM)] * 3,
+        scratch_shapes=[
+            pltpu.VMEM((rows, width), inputs.dtype),
+            pltpu.VMEM(words.shape, words.dtype),
+            pltpu.VMEM((width, rows), inputs.dtype),
+            pltpu.SemaphoreType.DMA,
+            pltpu.SemaphoreType.DMA,
+            pltpu.SemaphoreType.DMA,
+        ],
         compiler_params=params(6),
-        cost_estimate=cost(10**8, 4 * inputs.size),
-        name="unpack",
-    )(inputs, words)
+        cost_estimate=cost(10**8, 8 * inputs.size),
+        name="prepare",
+    )(*(pltpu.with_memory_space_constraint(value, pltpu.HBM) for value in (grads, inputs, words)))
 
 
 def token_sums_kernel(grads, inputs, scale, out):
@@ -173,8 +159,8 @@
     rows = saved_input.shape[0]
     order, order_aa = rotation(groups, FIRST_BA), rotation(planes, FIRST_AA)
 
-    arrived = exchange(arrange(grad_out.T, order), "ba", order)
-    by_device, scale = unpack(saved_input, keep_bits, order)
+    pieces, by_device, scale = prepare(grad_out.T, saved_input, keep_bits, order)
+    arrived = exchange(pieces, "ba", order)
     partial_sum = token_sums(arrived, by_device, scale)
     owned = jnp.sum(exchange(partial_sum[:, None, :], "ba", order), axis=0)
     copies = jnp.broadcast_to(owned[None], (planes, *owned.shape))

time: 76.4 us -> 74.9 us (0.980)
  blocking collectives: 12.6 us -> 55.6 us
  waiting for transfers between devices: 25.5 us -> 2.92 us
  starting transfers between devices: 29.6 us -> 8.26 us
    all_to_all x1 -> x2, blocking collectives: 12.6 us -> 55.6 us  [exchange(): lax.all_to_all(parts, axis, 0, 0, tiled=True, axis_index_groups=[order])]
    all_to_all x2 -> x1, waiting for transfers between devices: 25.5 us -> 2.92 us  [exchange(): lax.all_to_all(parts, axis, 0, 0, tiled=True, axis_index_groups=[order])]
    all_to_all x2 -> x1, starting transfers between devices: 29.6 us -> 8.26 us  [exchange(): lax.all_to_all(parts, axis, 0, 0, tiled=True, axis_index_groups=[order])]
    pallas_call x2 -> x1, Pallas kernels: 2.75 us -> 2.2 us  [prepare(): pl.pallas_call(functools.partial(prepare_kernel, order), out_shape=(jax.S...]
  transfers between devices with their start and end apart: 2 -> 1, of which waited for: 2 -> 1; matrix products, arithmetic and copies ran while one was open for 0% -> 0% of each run, Pallas kernels for 4% -> 3%
where the time goes in v3:
time: 74.9 us; the launch traced here: 74 us
  blocking collectives  55.6 us (74%)
  starting transfers between devices  8.26 us (11%)
  Pallas kernels  5.28 us (7%)
  waiting for transfers between devices  2.92 us (4%)
    all_to_all x2, blocking collectives, exchange(): lax.all_to_all(parts, axis, 0, 0, tiled=True, axis_index_groups=[order])  55.6 us
    all_to_all x1, starting transfers between devices, exchange(): lax.all_to_all(parts, axis, 0, 0, tiled=True, axis_index_groups=[order])  8.26 us
    all_to_all x1, waiting for transfers between devices, exchange(): lax.all_to_all(parts, axis, 0, 0, tiled=True, axis_index_groups=[order])  2.92 us
    pallas_call x1, Pallas kernels, input_grad(): pl.pallas_call(functools.partial(input_grad_kernel, order), out_shape=jax...  2.44 us
    pallas_call x1, Pallas kernels, prepare(): pl.pallas_call(functools.partial(prepare_kernel, order), out_shape=(jax.S...  2.2 us
  transfers between devices with their start and end apart: 1, of which 1 were waited for; matrix products, arithmetic and copies ran while one was open for 0% of the time, Pallas kernels for 3%

profile of v3, /device:TPU:1, one launch (start us, length us, event | category | flops | bytes accessed | tf_op | source)
XLA Modules:
  0.0 74.0 jit_solution(5547651089236506626)
XLA Ops:
  0.6 2.2 %prepare.1 = (bf16[64,64,128]{2,1,0:T(8,128)(2,1)S(1)}, bf16[64,64,128]{2,1,0:T(8,128)(2,1)S(1)}, f32[1,128]{1,0:T(1,128)S(1)}) custom-call(bf16[64,8192]{1,0:T(8,128)(2,1)} %bitcast.10, bf16[128,4096]{1,0:T(8,128)(2,1)} %inputs.3, s32[128,128]{1,0:T(8,128)} %words.3), custom_call_target="tpu_custom_call" | custom-call | flops 100000000 | bytes 4194304 | tf_op jit(solution)/shard_map/prepare/pallas_call | solution.py:78
  2.8 43.3 %all_to_all.15.grads = bf16[64,64,128]{2,1,0:T(8,128)(2,1)S(1)} all-to-all(bf16[64,64,128]{2,1,0:T(8,128)(2,1)S(1)} %get-tuple-element.5), channel_id=1, replica_groups={{37,38,39,40,41,42,43,44,45,46,47,48,49,50,51,52,53,54,55,56,57,58,59,6..., dimensions={0} | all-to-all | bytes 2097152 | tf_op jit(solution)/shard_map/all_to_all | solution.py:25
  46.1 0.0 copy-start
  46.1 0.6 token_sums.1
  46.8 0.0 copy-start.1
  46.8 12.3 %all_to_all.16 = f32[64,1,128]{2,1,0:T(1,128)S(1)} all-to-all(f32[64,1,128]{2,1,0:T(1,128)S(1)} %bitcast.8), channel_id=1, replica_groups={{37,38,39,40,41,42,43,44,45,46,47,48,49,50,51,52,53,54,55,56,57,58,59,6..., dimensions={0} | all-to-all | bytes 65536 | tf_op jit(solution)/shard_map/all_to_all | solution.py:25
  59.1 0.1 reduce_sum.20
  59.2 0.0 copy-start.2
  59.2 0.6 broadcast_in_dim.10
  59.8 8.3 %all-to-all-start.2 = ((f32[12,1,128]{2,1,0:T(1,128)}), f32[12,1,128]{2,1,0:T(1,128)S(1)}, u32[]{:S(2)}, u32[]{:S(2)}) async-start(f32[12,1,128]{2,1,0:T(1,128)} %broadcast_in_dim.10), calls=%async_computation.2 | async-start | bytes 12288 | tf_op jit(solution)/shard_map/all_to_all | solution.py:25
  68.0 0.0 copy-done
  68.0 0.0 copy-done.1
  68.0 0.0 copy-done.2
  68.0 2.4 %input_grad.1 = bf16[128,4096]{1,0:T(8,128)(2,1)} custom-call(bf16[64,64,128]{2,1,0:T(8,128)(2,1)S(1)} %all_to_all.15.grads, bf16[128,4096]{1,0:T(8,128)(2,1)S(1)} %copy-done, s32[128,128]{1,0:T(8,128)S(1)} %copy-done.1, f32[1,128]{1,0:T(1,128)S(1)} %get-tuple-element.6.scale, f32[1,4096]{1,0:T(1,128)S(1)} %bitcast.9), custom_call_target="tpu_custom_call" | custom-call | flops 100000000 | bytes 4194304 | tf_op jit(solution)/shard_map/input_grad/pallas_call | solution.py:146
  70.5 2.9 %all-to-all-done.2 = f32[12,1,128]{2,1,0:T(1,128)S(1)} async-done(((f32[12,1,128]{2,1,0:T(1,128)}), f32[12,1,128]{2,1,0:T(1,128)S(1)}, u32[]{:S(2)}, u32[]{:S(2)}) %all-to-all-start.2) | async-done | bytes 6176 | tf_op jit(solution)/shard_map/all_to_all | solution.py:25
  73.4 0.5 multiply_bitcast_fusion
  (1 shorter events, 0.0 us)
Async XLA Ops:
  46.1 21.9 %copy-start = (bf16[128,4096]{1,0:T(8,128)(2,1)S(1)}, bf16[128,4096]{1,0:T(8,128)(2,1)}, u32[]{:S(2)}) copy-start(bf16[128,4096]{1,0:T(8,128)(2,1)} %inputs.3) | copy-start | bytes 3145732
  46.8 21.3 %copy-start.1 = (s32[128,128]{1,0:T(8,128)S(1)}, s32[128,128]{1,0:T(8,128)}, u32[]{:S(2)}) copy-start(s32[128,128]{1,0:T(8,128)} %words.3) | copy-start | bytes 196612
  59.2 8.9 %copy-start.2 = (f32[4096]{0:T(1024)S(1)}, f32[4096]{0:T(1024)}, u32[]{:S(2)}) copy-start(f32[4096]{0:T(1024)} %param.7) | copy-start | bytes 49156
  59.8 13.6 %all-to-all-start.2 = ((f32[12,1,128]{2,1,0:T(1,128)}), f32[12,1,128]{2,1,0:T(1,128)S(1)}, u32[]{:S(2)}, u32[]{:S(2)}) async-start(f32[12,1,128]{2,1,0:T(1,128)} %broadcast_in_dim.10), calls=%async_computation.2 | async-start | bytes 12288 | tf_op jit(solution)/shard_map/all_to_all | solution.py:25

commit v4 on v3

--- a/solution.py
+++ b/solution.py
@@ -12,13 +12,15 @@
 EPSILON = 1e-06
 LANES = 128
 BITS = 32
-FIRST_BA = 37
-FIRST_AA = 9
+GRADS_ORDER = (37, 1)
+SUMS_ORDER = (37, 1)
+SHARES_ORDER = (9, 1)
+EARLY = 4
 F32 = jnp.float32
 
 
-def rotation(devices, first):
-    return [(first + i) % devices for i in range(devices)]
+def members(devices, first, step):
+    return [(first + i * step) % devices for i in range(devices)]
 
 
 def exchange(parts, axis, order):
@@ -97,19 +99,20 @@
     )(*(pltpu.with_memory_space_constraint(value, pltpu.HBM) for value in (grads, inputs, words)))
 
 
-def token_sums_kernel(grads, inputs, scale, out):
+def token_sums_kernel(order, out_order, grads, inputs, scale, out):
     devices, features, rows = grads.shape
     shape = (features, LANES)
     diagonal = lax.broadcasted_iota(jnp.int32, shape, 0) == lax.broadcasted_iota(jnp.int32, shape, 1)
     for d in range(devices):
         product = grads[d].astype(F32) * (inputs[d].astype(F32) * scale[...])
         sums = jnp.sum(product, axis=1, keepdims=True)
-        out[d : d + 1, :] = jnp.sum(jnp.where(diagonal, sums, 0.0), axis=0, keepdims=True)
-
-
-def token_sums(grads, inputs, scale):
+        row = out_order.index(order[d])
+        out[row : row + 1, :] = jnp.sum(jnp.where(diagonal, sums, 0.0), axis=0, keepdims=True)
+
+
+def token_sums(grads, inputs, scale, order, out_order):
     return pl.pallas_call(
-        token_sums_kernel,
+        functools.partial(token_sums_kernel, order, out_order),
         out_shape=jax.ShapeDtypeStruct((grads.shape[0], LANES), F32),
         compiler_params=params(6),
         cost_estimate=cost(10**7, 4 * grads.size),
@@ -117,8 +120,8 @@
     )(grads, inputs, scale)
 
 
-def input_grad_kernel(order, grads, inputs, words, scale, gain, out, scaled, normed, factor):
-    rows, width = out.shape
+def input_grad(order, grads, inputs, words, scale, gain, out, scaled, normed, factor):
+    rows, width = inputs.shape
     features = width // len(order)
     place = {device: i for i, device in enumerate(order)}
     words_t = words[...].T
@@ -141,35 +144,75 @@
         out[:, at] = value.astype(out.dtype)
 
 
-def input_grad(grads, inputs, words, scale, gain, order):
-    rows, width = inputs.shape
+def middle_kernel(order, parts, grads, inputs, words, scale, gain, copies, out, held, scaled, normed, factor, leave):
+    total = jnp.sum(parts[...], axis=0, keepdims=True)
+    copies[...] = jnp.broadcast_to(total[:, None, :], copies.shape)
+
+    @pl.when(lax.axis_index("aa") < EARLY)
+    def _():
+        input_grad(order, grads, inputs, words, scale, gain, held, scaled, normed, factor)
+        copy = pltpu.make_async_copy(held, out, leave)
+        copy.start()
+        copy.wait()
+
+
+def last_kernel(
+    order, norm, parts, grads, inputs, words, scale, gain, _, share, out, held, scaled, normed, factor, leave
+):
+    share[...] = jnp.sum(parts[...], axis=0)[:, : share.shape[1]] * norm
+
+    @pl.when(lax.axis_index("aa") >= EARLY)
+    def _():
+        input_grad(order, grads, inputs, words, scale, gain, held, scaled, normed, factor)
+        copy = pltpu.make_async_copy(held, out, leave)
+        copy.start()
+        copy.wait()
+
+
+def grad_call(kernel, operands, first_out, rows, width, aliased, name):
+    vmem, anywhere = pl.BlockSpec(memory_space=pltpu.VMEM), pl.BlockSpec(memory_space=pl.ANY)
+    count = len(operands)
     return pl.pallas_call(
-        functools.partial(input_grad_kernel, order),
-        out_shape=jax.ShapeDtypeStruct((rows, width), inputs.dtype),
-        scratch_shapes=[pltpu.VMEM((rows, width), F32)] * 3,
+        kernel,
+        out_shape=(first_out, jax.ShapeDtypeStruct((rows, width), jnp.bfloat16)),
+        in_specs=[vmem] * (count - aliased) + [anywhere] * aliased,
+        out_specs=(vmem, anywhere),
+        scratch_shapes=[pltpu.VMEM((rows, width), jnp.bfloat16)]
+        + [pltpu.VMEM((rows, width), F32)] * 3
+        + [pltpu.SemaphoreType.DMA],
+        input_output_aliases={count - 1: 1} if aliased else {},
         compiler_params=params(14),
-        cost_estimate=cost(10**8, 8 * inputs.size),
-        name="input_grad",
-    )(grads, inputs, words, scale, gain.reshape(1, width))
+        cost_estimate=cost(10**8, 8 * rows * width),
+        name=name,
+    )(*operands)
 
 
 def per_device(grad_out, saved_input, keep_bits, gain):
     groups, planes = lax.axis_size("ba"), lax.axis_size("aa")
     features = grad_out.shape[1]
-    rows = saved_input.shape[0]
-    order, order_aa = rotation(groups, FIRST_BA), rotation(planes, FIRST_AA)
+    rows, width = saved_input.shape
+    order, sums_order = members(groups, *GRADS_ORDER), members(groups, *SUMS_ORDER)
 
     pieces, by_device, scale = prepare(grad_out.T, saved_input, keep_bits, order)
     arrived = exchange(pieces, "ba", order)
-    partial_sum = token_sums(arrived, by_device, scale)
-    owned = jnp.sum(exchange(partial_sum[:, None, :], "ba", order), axis=0)
-    copies = jnp.broadcast_to(owned[None], (planes, *owned.shape))
-    share = jnp.sum(exchange(copies, "aa", order_aa), axis=0).reshape(-1)[:features]
-    gain_grad = share * (1.0 / math.sqrt(rows * groups * planes))
-
-    late, _ = lax.optimization_barrier((arrived, owned))
-    grad_in = input_grad(late, saved_input, keep_bits, scale, gain, order)
-    return (grad_in, gain_grad)
+    sums = token_sums(arrived, by_device, scale, order, sums_order)
+    sums = exchange(sums[:, None, :], "ba", sums_order)
+
+    local = (arrived, saved_input, keep_bits, scale, gain.reshape(1, width))
+    copies, grad_in = grad_call(
+        functools.partial(middle_kernel, order),
+        (sums.reshape(groups, LANES), *local),
+        jax.ShapeDtypeStruct((planes, 1, LANES), F32),
+        rows, width, 0, "middle",
+    )
+    shares = exchange(copies, "aa", members(planes, *SHARES_ORDER))
+    share, grad_in = grad_call(
+        functools.partial(last_kernel, order, 1.0 / math.sqrt(rows * groups * planes)),
+        (shares, *local, grad_in),
+        jax.ShapeDtypeStruct((1, features), F32),
+        rows, width, 1, "last",
+    )
+    return (grad_in, share.reshape(features))
 
 
 def solution(mesh):

time: 74.9 us -> 74 us (0.988)
  blocking collectives: 55.6 us -> 66.5 us
  starting transfers between devices: 8.26 us -> 0 us
  waiting for transfers between devices: 2.92 us -> 0 us
    all_to_all x2 -> x3, blocking collectives: 55.6 us -> 66.5 us  [exchange(): lax.all_to_all(parts, axis, 0, 0, tiled=True, axis_index_groups=[order])]
    all_to_all x1 -> x0, starting transfers between devices: 8.26 us -> none  [exchange(): lax.all_to_all(parts, axis, 0, 0, tiled=True, axis_index_groups=[order])]
    all_to_all x1 -> x0, waiting for transfers between devices: 2.92 us -> none  [exchange(): lax.all_to_all(parts, axis, 0, 0, tiled=True, axis_index_groups=[order])]
    pallas_call x2 -> x3, Pallas kernels: 3.08 us -> 3.69 us  [the longest x2 3.05 us: grad_call(): pl.pallas_call(kernel, out_shape=(first_out, jax.ShapeDtypeStruct((rows,...]
  transfers between devices with their start and end apart: 1 -> 0, of which waited for: 1 -> 0; matrix products, arithmetic and copies ran while one was open for 0% -> 0% of each run, Pallas kernels for 3% -> 0%
where the time goes in v4:
time: 74 us; the launch traced here: 73.1 us
  blocking collectives  66.5 us (90%)
  Pallas kernels  5.9 us (8%)
    all_to_all x3, blocking collectives, exchange(): lax.all_to_all(parts, axis, 0, 0, tiled=True, axis_index_groups=[order])  66.5 us
    pallas_call x2, Pallas kernels, grad_call(): pl.pallas_call(kernel, out_shape=(first_out, jax.ShapeDtypeStruct((rows,...  3.05 us
    pallas_call x1, Pallas kernels, prepare(): pl.pallas_call(functools.partial(prepare_kernel, order), out_shape=(jax.S...  2.2 us

profile of v4, /device:TPU:1, one launch (start us, length us, event | category | flops | bytes accessed | tf_op | source)
XLA Modules:
  0.0 73.1 jit_solution(12161218958159254338)
XLA Ops:
  0.6 2.2 %prepare.1 = (bf16[64,64,128]{2,1,0:T(8,128)(2,1)S(1)}, bf16[64,64,128]{2,1,0:T(8,128)(2,1)S(1)}, f32[1,128]{1,0:T(1,128)S(1)}) custom-call(bf16[64,8192]{1,0:T(8,128)(2,1)} %bitcast.11, bf16[128,4096]{1,0:T(8,128)(2,1)} %inputs.5, s32[128,128]{1,0:T(8,128)} %words.5), custom_call_target="tpu_custom_call" | custom-call | flops 100000000 | bytes 4194304 | tf_op jit(solution)/shard_map/prepare/pallas_call | solution.py:80
  2.8 43.3 %all_to_all.15.grads = bf16[64,64,128]{2,1,0:T(8,128)(2,1)S(1)} all-to-all(bf16[64,64,128]{2,1,0:T(8,128)(2,1)S(1)} %get-tuple-element.9), channel_id=1, replica_groups={{37,38,39,40,41,42,43,44,45,46,47,48,49,50,51,52,53,54,55,56,57,58,59,6..., dimensions={0} | all-to-all | bytes 2097152 | tf_op jit(solution)/shard_map/all_to_all | solution.py:27
  46.1 0.0 copy-start
  46.1 0.0 copy-start.2
  46.1 0.6 token_sums.1
  46.8 0.0 copy-start.1
  46.8 12.3 %all_to_all.16 = f32[64,1,128]{2,1,0:T(1,128)S(1)} all-to-all(f32[64,1,128]{2,1,0:T(1,128)S(1)} %bitcast.8), channel_id=1, replica_groups={{37,38,39,40,41,42,43,44,45,46,47,48,49,50,51,52,53,54,55,56,57,58,59,6..., dimensions={0} | all-to-all | bytes 65536 | tf_op jit(solution)/shard_map/all_to_all | solution.py:27
  59.1 0.0 copy-done
  59.1 0.0 copy-done.2
  59.1 0.0 copy-done.1
  59.1 2.5 %middle.1 = (f32[12,1,128]{2,1,0:T(1,128)S(1)}, bf16[128,4096]{1,0:T(8,128)(2,1)}) custom-call(f32[64,128]{1,0:T(8,128)S(1)} %bitcast.7, bf16[64,64,128]{2,1,0:T(8,128)(2,1)S(1)} %all_to_all.15.grads, bf16[128,4096]{1,0:T(8,128)(2,1)S(1)} %copy-done, s32[128,128]{1,0:T(8,128)S(1)} %copy-done.1, f32[1,128]{1,0:T(1,128)S(1)} %get-tuple-element.11.scale, ...), custom_call_target="tpu_custom_call" | custom-call | flops 100000000 | bytes 4194304 | tf_op jit(solution)/shard_map/middle/pallas_call | solution.py:175
  61.6 11.0 %all_to_all.17.parts = f32[12,1,128]{2,1,0:T(1,128)S(1)} all-to-all(f32[12,1,128]{2,1,0:T(1,128)S(1)} %get-tuple-element.12), channel_id=1, replica_groups={{576,640,704,0,64,128,192,256,320,384,448,512},{577,641,705,1,65,129,19..., dimensions={0} | all-to-all | bytes 12288 | tf_op jit(solution)/shard_map/all_to_all | solution.py:27
  72.6 0.5 last.1
Async XLA Ops:
  46.1 13.0 %copy-start = (bf16[128,4096]{1,0:T(8,128)(2,1)S(1)}, bf16[128,4096]{1,0:T(8,128)(2,1)}, u32[]{:S(2)}) copy-start(bf16[128,4096]{1,0:T(8,128)(2,1)} %inputs.5) | copy-start | bytes 3145732
  46.1 13.0 %copy-start.2 = (f32[4096]{0:T(1024)S(1)}, f32[4096]{0:T(1024)}, u32[]{:S(2)}) copy-start(f32[4096]{0:T(1024)} %param.7) | copy-start | bytes 49156
  46.8 12.3 %copy-start.1 = (s32[128,128]{1,0:T(8,128)S(1)}, s32[128,128]{1,0:T(8,128)}, u32[]{:S(2)}) copy-start(s32[128,128]{1,0:T(8,128)} %words.5) | copy-start | bytes 196612

commit v5 on v4

--- a/solution.py
+++ b/solution.py
@@ -12,15 +12,11 @@
 EPSILON = 1e-06
 LANES = 128
 BITS = 32
-GRADS_ORDER = (37, 1)
-SUMS_ORDER = (37, 1)
-SHARES_ORDER = (9, 1)
+GRADS_ORDER = [(37 + i) % 64 for i in range(64)]
+SUMS_ORDER = [(37 + i) % 64 for i in range(64)]
+SHARES_ORDER = [(9 + i) % 12 for i in range(12)]
 EARLY = 4
 F32 = jnp.float32
-
-
-def members(devices, first, step):
-    return [(first + i * step) % devices for i in range(devices)]
 
 
 def exchange(parts, axis, order):
@@ -52,6 +48,7 @@
     rows_copy = pltpu.make_async_copy(inputs, rows_in, rows_sem)
     words_copy.start()
     rows_copy.start()
+    pl.delay(100)
     for i, device in enumerate(order):
         pltpu.make_async_copy(grads.at[:, pl.ds(device * rows, rows)], pieces.at[i], move).start()
     words_copy.wait()
@@ -64,11 +61,11 @@
     for q in range(width // LANES):
         at = slice(q * LANES, (q + 1) * LANES)
         value = rows_in[:, at].T * kept[at, :]
-        dropped = value.astype(F32) * (1.0 / KEEP_RATE)
-        squares += jnp.sum((dropped * dropped).reshape(LANES // 8, 8, rows), axis=0)
+        kept_value = value.astype(F32)
+        squares += jnp.sum((kept_value * kept_value).reshape(LANES // 8, 8, rows), axis=0)
         for h in range(LANES // features):
             by_device[place[q * LANES // features + h]] = value[h * features : (h + 1) * features, :]
-    mean = jnp.sum(squares, axis=0, keepdims=True) * (1.0 / width)
+    mean = jnp.sum(squares, axis=0, keepdims=True) * (1.0 / (KEEP_RATE * KEEP_RATE * width))
     scale[...] = lax.rsqrt(mean + EPSILON) * (1.0 / KEEP_RATE)
     pltpu.make_async_copy(pieces, pieces, move).wait()
 
@@ -191,7 +188,7 @@
     groups, planes = lax.axis_size("ba"), lax.axis_size("aa")
     features = grad_out.shape[1]
     rows, width = saved_input.shape
-    order, sums_order = members(groups, *GRADS_ORDER), members(groups, *SUMS_ORDER)
+    order, sums_order = GRADS_ORDER, SUMS_ORDER
 
     pieces, by_device, scale = prepare(grad_out.T, saved_input, keep_bits, order)
     arrived = exchange(pieces, "ba", order)
@@ -205,7 +202,7 @@
         jax.ShapeDtypeStruct((planes, 1, LANES), F32),
         rows, width, 0, "middle",
     )
-    shares = exchange(copies, "aa", members(planes, *SHARES_ORDER))
+    shares = exchange(copies, "aa", SHARES_ORDER)
     share, grad_in = grad_call(
         functools.partial(last_kernel, order, 1.0 / math.sqrt(rows * groups * planes)),
         (shares, *local, grad_in),

time: 74 us -> 73.5 us (level)
  no operation moved by 1% of the time
where the time goes in v5:
time: 73.5 us; the launch traced here: 72.6 us
  blocking collectives  66.5 us (90%)
  Pallas kernels  5.41 us (7%)
    all_to_all x3, blocking collectives, exchange(): lax.all_to_all(parts, axis, 0, 0, tiled=True, axis_index_groups=[order])  66.5 us
    pallas_call x2, Pallas kernels, grad_call(): pl.pallas_call(kernel, out_shape=(first_out, jax.ShapeDtypeStruct((rows,...  3.05 us
    pallas_call x1, Pallas kernels, prepare(): pl.pallas_call(functools.partial(prepare_kernel, order), out_shape=(jax.S...  1.71 us

profile of v5, /device:TPU:1, one launch (start us, length us, event | category | flops | bytes accessed | tf_op | source)
XLA Modules:
  0.0 72.6 jit_solution(1173327885007775764)
XLA Ops:
  0.6 1.7 %prepare.1 = (bf16[64,64,128]{2,1,0:T(8,128)(2,1)S(1)}, bf16[64,64,128]{2,1,0:T(8,128)(2,1)S(1)}, f32[1,128]{1,0:T(1,128)S(1)}) custom-call(bf16[64,8192]{1,0:T(8,128)(2,1)} %bitcast.11, bf16[128,4096]{1,0:T(8,128)(2,1)} %inputs.5, s32[128,128]{1,0:T(8,128)} %words.5), custom_call_target="tpu_custom_call" | custom-call | flops 100000000 | bytes 4194304 | tf_op jit(solution)/shard_map/prepare/pallas_call | solution.py:77
  2.4 43.3 %all_to_all.15.grads = bf16[64,64,128]{2,1,0:T(8,128)(2,1)S(1)} all-to-all(bf16[64,64,128]{2,1,0:T(8,128)(2,1)S(1)} %get-tuple-element.9), channel_id=1, replica_groups={{37,38,39,40,41,42,43,44,45,46,47,48,49,50,51,52,53,54,55,56,57,58,59,6..., dimensions={0} | all-to-all | bytes 2097152 | tf_op jit(solution)/shard_map/all_to_all | solution.py:23
  45.6 0.0 copy-start
  45.6 0.0 copy-start.2
  45.6 0.6 token_sums.1
  46.3 0.0 copy-start.1
  46.3 12.3 %all_to_all.16 = f32[64,1,128]{2,1,0:T(1,128)S(1)} all-to-all(f32[64,1,128]{2,1,0:T(1,128)S(1)} %bitcast.8), channel_id=1, replica_groups={{37,38,39,40,41,42,43,44,45,46,47,48,49,50,51,52,53,54,55,56,57,58,59,6..., dimensions={0} | all-to-all | bytes 65536 | tf_op jit(solution)/shard_map/all_to_all | solution.py:23
  58.6 0.0 copy-done
  58.6 0.0 copy-done.2
  58.6 0.0 copy-done.1
  58.6 2.5 %middle.1 = (f32[12,1,128]{2,1,0:T(1,128)S(1)}, bf16[128,4096]{1,0:T(8,128)(2,1)}) custom-call(f32[64,128]{1,0:T(8,128)S(1)} %bitcast.7, bf16[64,64,128]{2,1,0:T(8,128)(2,1)S(1)} %all_to_all.15.grads, bf16[128,4096]{1,0:T(8,128)(2,1)S(1)} %copy-done, s32[128,128]{1,0:T(8,128)S(1)} %copy-done.1, f32[1,128]{1,0:T(1,128)S(1)} %get-tuple-element.11.scale, ...), custom_call_target="tpu_custom_call" | custom-call | flops 100000000 | bytes 4194304 | tf_op jit(solution)/shard_map/middle/pallas_call | solution.py:172
  61.1 11.0 %all_to_all.17.parts = f32[12,1,128]{2,1,0:T(1,128)S(1)} all-to-all(f32[12,1,128]{2,1,0:T(1,128)S(1)} %get-tuple-element.12), channel_id=1, replica_groups={{576,640,704,0,64,128,192,256,320,384,448,512},{577,641,705,1,65,129,19..., dimensions={0} | all-to-all | bytes 12288 | tf_op jit(solution)/shard_map/all_to_all | solution.py:23
  72.1 0.5 last.1
Async XLA Ops:
  45.6 13.0 %copy-start = (bf16[128,4096]{1,0:T(8,128)(2,1)S(1)}, bf16[128,4096]{1,0:T(8,128)(2,1)}, u32[]{:S(2)}) copy-start(bf16[128,4096]{1,0:T(8,128)(2,1)} %inputs.5) | copy-start | bytes 3145732
  45.6 13.0 %copy-start.2 = (f32[4096]{0:T(1024)S(1)}, f32[4096]{0:T(1024)}, u32[]{:S(2)}) copy-start(f32[4096]{0:T(1024)} %param.7) | copy-start | bytes 49156
  46.3 12.3 %copy-start.1 = (s32[128,128]{1,0:T(8,128)S(1)}, s32[128,128]{1,0:T(8,128)}, u32[]{:S(2)}) copy-start(s32[128,128]{1,0:T(8,128)} %words.5) | copy-start | bytes 196612

commit v6 on v5

--- a/solution.py
+++ b/solution.py
@@ -15,12 +15,18 @@
 GRADS_ORDER = [(37 + i) % 64 for i in range(64)]
 SUMS_ORDER = [(37 + i) % 64 for i in range(64)]
 SHARES_ORDER = [(9 + i) % 12 for i in range(12)]
+SWAPPED = (3, 4, 5, 6, 7, 9, 10)
+CORES = 2
 EARLY = 4
 F32 = jnp.float32
 
 
-def exchange(parts, axis, order):
-    return lax.all_to_all(parts, axis, 0, 0, tiled=True, axis_index_groups=[order])
+def exchange(parts, axis, groups):
+    return lax.all_to_all(parts, axis, 0, 0, tiled=True, axis_index_groups=groups)
+
+
+def swaps(plane, device):
+    return plane in SWAPPED and device >= CORES
 
 
 def params(mib):
@@ -98,13 +104,18 @@
 
 def token_sums_kernel(order, out_order, grads, inputs, scale, out):
     devices, features, rows = grads.shape
-    shape = (features, LANES)
-    diagonal = lax.broadcasted_iota(jnp.int32, shape, 0) == lax.broadcasted_iota(jnp.int32, shape, 1)
-    for d in range(devices):
-        product = grads[d].astype(F32) * (inputs[d].astype(F32) * scale[...])
-        sums = jnp.sum(product, axis=1, keepdims=True)
-        row = out_order.index(order[d])
-        out[row : row + 1, :] = jnp.sum(jnp.where(diagonal, sums, 0.0), axis=0, keepdims=True)
+    row = lax.broadcasted_iota(jnp.int32, (features, LANES), 0)
+    lane = lax.broadcasted_iota(jnp.int32, (features, LANES), 1)
+    for first in range(0, devices, CORES):
+        chip = jnp.zeros((1, LANES), F32)
+        for core in range(CORES):
+            d = order.index(first + core)
+            product = grads[d].astype(F32) * (inputs[d].astype(F32) * scale[...])
+            sums = jnp.sum(product, axis=1, keepdims=True)
+            chip += jnp.sum(jnp.where(row == lane - core * features, sums, 0.0), axis=0, keepdims=True)
+        for core in range(CORES):
+            at = out_order.index(first + core)
+            out[at : at + 1, :] = chip
 
 
 def token_sums(grads, inputs, scale, order, out_order):
@@ -156,7 +167,10 @@
 def last_kernel(
     order, norm, parts, grads, inputs, words, scale, gain, _, share, out, held, scaled, normed, factor, leave
 ):
-    share[...] = jnp.sum(parts[...], axis=0)[:, : share.shape[1]] * norm
+    total = jnp.sum(parts[...], axis=0) * norm
+    features = share.shape[1]
+    first, second = total[:, :features], pltpu.roll(total, LANES - features, 1)[:, :features]
+    share[...] = jnp.where(lax.axis_index("ba") % CORES == 0, first, second)
 
     @pl.when(lax.axis_index("aa") >= EARLY)
     def _():
@@ -191,9 +205,9 @@
     order, sums_order = GRADS_ORDER, SUMS_ORDER
 
     pieces, by_device, scale = prepare(grad_out.T, saved_input, keep_bits, order)
-    arrived = exchange(pieces, "ba", order)
+    arrived = exchange(pieces, "ba", [order])
     sums = token_sums(arrived, by_device, scale, order, sums_order)
-    sums = exchange(sums[:, None, :], "ba", sums_order)
+    sums = exchange(sums[:, None, :], "ba", [sums_order])
 
     local = (arrived, saved_input, keep_bits, scale, gain.reshape(1, width))
     copies, grad_in = grad_call(
@@ -202,7 +216,8 @@
         jax.ShapeDtypeStruct((planes, 1, LANES), F32),
         rows, width, 0, "middle",
     )
-    shares = exchange(copies, "aa", SHARES_ORDER)
+    members = [[(z, d + 1 - 2 * (d % CORES) if swaps(z, d) else d) for z in SHARES_ORDER] for d in range(groups)]
+    shares = exchange(copies, ("aa", "ba"), [[z * groups + d for z, d in group] for group in members])
     share, grad_in = grad_call(
         functools.partial(last_kernel, order, 1.0 / math.sqrt(rows * groups * planes)),
         (shares, *local, grad_in),

time: 73.5 us -> 73 us (level)
  no operation moved by 1% of the time
where the time goes in v6:
time: 73 us; the launch traced here: 72.7 us
  blocking collectives  66.5 us (91%)
  Pallas kernels  5.47 us (7%)
    all_to_all x3, blocking collectives, exchange(): lax.all_to_all(parts, axis, 0, 0, tiled=True, axis_index_groups=groups)  66.5 us
    pallas_call x2, Pallas kernels, grad_call(): pl.pallas_call(kernel, out_shape=(first_out, jax.ShapeDtypeStruct((rows,...  3.12 us
    pallas_call x1, Pallas kernels, prepare(): pl.pallas_call(functools.partial(prepare_kernel, order), out_shape=(jax.S...  1.71 us

profile of v6, /device:TPU:1, one launch (start us, length us, event | category | flops | bytes accessed | tf_op | source)
XLA Modules:
  0.0 72.7 jit_solution(334179716249112066)
XLA Ops:
  0.6 1.7 %prepare.1 = (bf16[64,64,128]{2,1,0:T(8,128)(2,1)S(1)}, bf16[64,64,128]{2,1,0:T(8,128)(2,1)S(1)}, f32[1,128]{1,0:T(1,128)S(1)}) custom-call(bf16[64,8192]{1,0:T(8,128)(2,1)} %bitcast.11, bf16[128,4096]{1,0:T(8,128)(2,1)} %inputs.5, s32[128,128]{1,0:T(8,128)} %words.5), custom_call_target="tpu_custom_call" | custom-call | flops 100000000 | bytes 4194304 | tf_op jit(solution)/shard_map/prepare/pallas_call | solution.py:83
  2.4 43.3 %all_to_all.15.grads = bf16[64,64,128]{2,1,0:T(8,128)(2,1)S(1)} all-to-all(bf16[64,64,128]{2,1,0:T(8,128)(2,1)S(1)} %get-tuple-element.9), channel_id=1, replica_groups={{37,38,39,40,41,42,43,44,45,46,47,48,49,50,51,52,53,54,55,56,57,58,59,6..., dimensions={0} | all-to-all | bytes 2097152 | tf_op jit(solution)/shard_map/all_to_all | solution.py:25
  45.6 0.0 copy-start
  45.6 0.0 copy-start.2
  45.6 0.6 token_sums.1
  46.3 0.0 copy-start.1
  46.3 12.3 %all_to_all.16 = f32[64,1,128]{2,1,0:T(1,128)S(1)} all-to-all(f32[64,1,128]{2,1,0:T(1,128)S(1)} %bitcast.8), channel_id=1, replica_groups={{37,38,39,40,41,42,43,44,45,46,47,48,49,50,51,52,53,54,55,56,57,58,59,6..., dimensions={0} | all-to-all | bytes 65536 | tf_op jit(solution)/shard_map/all_to_all | solution.py:25
  58.6 0.0 copy-done
  58.6 0.0 copy-done.2
  58.6 0.0 copy-done.1
  58.6 2.5 %middle.1 = (f32[12,1,128]{2,1,0:T(1,128)S(1)}, bf16[128,4096]{1,0:T(8,128)(2,1)}) custom-call(f32[64,128]{1,0:T(8,128)S(1)} %bitcast.7, bf16[64,64,128]{2,1,0:T(8,128)(2,1)S(1)} %all_to_all.15.grads, bf16[128,4096]{1,0:T(8,128)(2,1)S(1)} %copy-done, s32[128,128]{1,0:T(8,128)S(1)} %copy-done.1, f32[1,128]{1,0:T(1,128)S(1)} %get-tuple-element.11.scale, ...), custom_call_target="tpu_custom_call" | custom-call | flops 100000000 | bytes 4194304 | tf_op jit(solution)/shard_map/middle/pallas_call | solution.py:186
  61.1 11.0 %all_to_all.17.parts = f32[12,1,128]{2,1,0:T(1,128)S(1)} all-to-all(f32[12,1,128]{2,1,0:T(1,128)S(1)} %get-tuple-element.12), channel_id=1, replica_groups={{576,640,704,0,64,128,192,256,320,384,448,512},{577,641,705,1,65,129,19..., dimensions={0} | all-to-all | bytes 12288 | tf_op jit(solution)/shard_map/all_to_all | solution.py:25
  72.1 0.6 last.1
Async XLA Ops:
  45.6 13.0 %copy-start = (bf16[128,4096]{1,0:T(8,128)(2,1)S(1)}, bf16[128,4096]{1,0:T(8,128)(2,1)}, u32[]{:S(2)}) copy-start(bf16[128,4096]{1,0:T(8,128)(2,1)} %inputs.5) | copy-start | bytes 3145732
  45.6 13.0 %copy-start.2 = (f32[4096]{0:T(1024)S(1)}, f32[4096]{0:T(1024)}, u32[]{:S(2)}) copy-start(f32[4096]{0:T(1024)} %param.7) | copy-start | bytes 49156
  46.3 12.3 %copy-start.1 = (s32[128,128]{1,0:T(8,128)S(1)}, s32[128,128]{1,0:T(8,128)}, u32[]{:S(2)}) copy-start(s32[128,128]{1,0:T(8,128)} %words.5) | copy-start | bytes 196612

commit v7 on v6

--- a/solution.py
+++ b/solution.py
@@ -14,8 +14,9 @@
 BITS = 32
 GRADS_ORDER = [(37 + i) % 64 for i in range(64)]
 SUMS_ORDER = [(37 + i) % 64 for i in range(64)]
-SHARES_ORDER = [(9 + i) % 12 for i in range(12)]
-SWAPPED = (3, 4, 5, 6, 7, 9, 10)
+FIRST_PLANES = (9, 8)
+SHARES_ORDERS = [[(first + i) % 12 for i in range(12)] for first in FIRST_PLANES]
+SWAPPED = (3, 4, 5, 6, 9)
 CORES = 2
 EARLY = 4
 F32 = jnp.float32
@@ -216,7 +217,10 @@
         jax.ShapeDtypeStruct((planes, 1, LANES), F32),
         rows, width, 0, "middle",
     )
-    members = [[(z, d + 1 - 2 * (d % CORES) if swaps(z, d) else d) for z in SHARES_ORDER] for d in range(groups)]
+    members = [
+        [(z, d + 1 - 2 * (d % CORES) if swaps(z, d) else d) for z in SHARES_ORDERS[d % CORES]]
+        for d in range(groups)
+    ]
     shares = exchange(copies, ("aa", "ba"), [[z * groups + d for z, d in group] for group in members])
     share, grad_in = grad_call(
         functools.partial(last_kernel, order, 1.0 / math.sqrt(rows * groups * planes)),

time: 73 us -> 72.9 us (level)
  no operation moved by 1% of the time
where the time goes in v7:
time: 72.9 us; the launch traced here: 72.7 us
  blocking collectives  66.5 us (91%)
  Pallas kernels  5.47 us (8%)
    all_to_all x3, blocking collectives, exchange(): lax.all_to_all(parts, axis, 0, 0, tiled=True, axis_index_groups=groups)  66.5 us
    pallas_call x2, Pallas kernels, grad_call(): pl.pallas_call(kernel, out_shape=(first_out, jax.ShapeDtypeStruct((rows,...  3.12 us
    pallas_call x1, Pallas kernels, prepare(): pl.pallas_call(functools.partial(prepare_kernel, order), out_shape=(jax.S...  1.71 us

profile of v7, /device:TPU:1, one launch (start us, length us, event | category | flops | bytes accessed | tf_op | source)
XLA Modules:
  0.0 72.7 jit_solution(7373955537566012589)
XLA Ops:
  0.6 1.7 %prepare.1 = (bf16[64,64,128]{2,1,0:T(8,128)(2,1)S(1)}, bf16[64,64,128]{2,1,0:T(8,128)(2,1)S(1)}, f32[1,128]{1,0:T(1,128)S(1)}) custom-call(bf16[64,8192]{1,0:T(8,128)(2,1)} %bitcast.11, bf16[128,4096]{1,0:T(8,128)(2,1)} %inputs.5, s32[128,128]{1,0:T(8,128)} %words.5), custom_call_target="tpu_custom_call" | custom-call | flops 100000000 | bytes 4194304 | tf_op jit(solution)/shard_map/prepare/pallas_call | solution.py:84
  2.4 43.3 %all_to_all.15.grads = bf16[64,64,128]{2,1,0:T(8,128)(2,1)S(1)} all-to-all(bf16[64,64,128]{2,1,0:T(8,128)(2,1)S(1)} %get-tuple-element.9), channel_id=1, replica_groups={{37,38,39,40,41,42,43,44,45,46,47,48,49,50,51,52,53,54,55,56,57,58,59,6..., dimensions={0} | all-to-all | bytes 2097152 | tf_op jit(solution)/shard_map/all_to_all | solution.py:26
  45.6 0.0 copy-start
  45.6 0.0 copy-start.2
  45.6 0.6 token_sums.1
  46.3 0.0 copy-start.1
  46.3 12.3 %all_to_all.16 = f32[64,1,128]{2,1,0:T(1,128)S(1)} all-to-all(f32[64,1,128]{2,1,0:T(1,128)S(1)} %bitcast.8), channel_id=1, replica_groups={{37,38,39,40,41,42,43,44,45,46,47,48,49,50,51,52,53,54,55,56,57,58,59,6..., dimensions={0} | all-to-all | bytes 65536 | tf_op jit(solution)/shard_map/all_to_all | solution.py:26
  58.6 0.0 copy-done
  58.6 0.0 copy-done.2
  58.6 0.0 copy-done.1
  58.6 2.5 %middle.1 = (f32[12,1,128]{2,1,0:T(1,128)S(1)}, bf16[128,4096]{1,0:T(8,128)(2,1)}) custom-call(f32[64,128]{1,0:T(8,128)S(1)} %bitcast.7, bf16[64,64,128]{2,1,0:T(8,128)(2,1)S(1)} %all_to_all.15.grads, bf16[128,4096]{1,0:T(8,128)(2,1)S(1)} %copy-done, s32[128,128]{1,0:T(8,128)S(1)} %copy-done.1, f32[1,128]{1,0:T(1,128)S(1)} %get-tuple-element.11.scale, ...), custom_call_target="tpu_custom_call" | custom-call | flops 100000000 | bytes 4194304 | tf_op jit(solution)/shard_map/middle/pallas_call | solution.py:187
  61.1 11.0 %all_to_all.17.parts = f32[12,1,128]{2,1,0:T(1,128)S(1)} all-to-all(f32[12,1,128]{2,1,0:T(1,128)S(1)} %get-tuple-element.12), channel_id=1, replica_groups={{576,640,704,0,64,128,192,256,320,384,448,512},{513,577,641,705,1,65,12..., dimensions={0} | all-to-all | bytes 12288 | tf_op jit(solution)/shard_map/all_to_all | solution.py:26
  72.1 0.6 last.1
Async XLA Ops:
  45.6 13.0 %copy-start = (bf16[128,4096]{1,0:T(8,128)(2,1)S(1)}, bf16[128,4096]{1,0:T(8,128)(2,1)}, u32[]{:S(2)}) copy-start(bf16[128,4096]{1,0:T(8,128)(2,1)} %inputs.5) | copy-start | bytes 3145732
  45.6 13.0 %copy-start.2 = (f32[4096]{0:T(1024)S(1)}, f32[4096]{0:T(1024)}, u32[]{:S(2)}) copy-start(f32[4096]{0:T(1024)} %param.7) | copy-start | bytes 49156
  46.3 12.3 %copy-start.1 = (s32[128,128]{1,0:T(8,128)S(1)}, s32[128,128]{1,0:T(8,128)}, u32[]{:S(2)}) copy-start(s32[128,128]{1,0:T(8,128)} %words.5) | copy-start | bytes 196612

commit v8 on v7

--- a/solution.py
+++ b/solution.py
@@ -87,11 +87,11 @@
             jax.ShapeDtypeStruct(shape, grads.dtype),
             jax.ShapeDtypeStruct(shape, inputs.dtype),
             jax.ShapeDtypeStruct((1, rows), F32),
+            jax.ShapeDtypeStruct(inputs.shape, inputs.dtype),
+            jax.ShapeDtypeStruct(words.shape, words.dtype),
         ),
         in_specs=[pl.BlockSpec(memory_space=pltpu.HBM)] * 3,
         scratch_shapes=[
-            pltpu.VMEM((rows, width), inputs.dtype),
-            pltpu.VMEM(words.shape, words.dtype),
             pltpu.VMEM((width, rows), inputs.dtype),
             pltpu.SemaphoreType.DMA,
             pltpu.SemaphoreType.DMA,
@@ -205,12 +205,12 @@
     rows, width = saved_input.shape
     order, sums_order = GRADS_ORDER, SUMS_ORDER
 
-    pieces, by_device, scale = prepare(grad_out.T, saved_input, keep_bits, order)
+    pieces, by_device, scale, inputs, words = prepare(grad_out.T, saved_input, keep_bits, order)
     arrived = exchange(pieces, "ba", [order])
     sums = token_sums(arrived, by_device, scale, order, sums_order)
     sums = exchange(sums[:, None, :], "ba", [sums_order])
 
-    local = (arrived, saved_input, keep_bits, scale, gain.reshape(1, width))
+    local = (arrived, inputs, words, scale, gain.reshape(1, width))
     copies, grad_in = grad_call(
         functools.partial(middle_kernel, order),
         (sums.reshape(groups, LANES), *local),

time: 72.9 us -> 73 us (level)
  no operation moved by 1% of the time
where the time goes in v8:
time: 73 us; the launch traced here: 72.7 us
  blocking collectives  66.5 us (91%)
  Pallas kernels  5.48 us (8%)
    all_to_all x3, blocking collectives, exchange(): lax.all_to_all(parts, axis, 0, 0, tiled=True, axis_index_groups=groups)  66.5 us
    pallas_call x2, Pallas kernels, grad_call(): pl.pallas_call(kernel, out_shape=(first_out, jax.ShapeDtypeStruct((rows,...  3.12 us
    pallas_call x1, Pallas kernels, prepare(): pl.pallas_call(functools.partial(prepare_kernel, order), out_shape=(jax.S...  1.73 us

profile of v8, /device:TPU:1, one launch (start us, length us, event | category | flops | bytes accessed | tf_op | source)
XLA Modules:
  0.0 72.7 jit_solution(15662759317894633930)
XLA Ops:
  0.6 1.7 %prepare.1 = (bf16[64,64,128]{2,1,0:T(8,128)(2,1)S(1)}, bf16[64,64,128]{2,1,0:T(8,128)(2,1)S(1)}, f32[1,128]{1,0:T(1,128)S(1)}, bf16[128,4096]{1,0:T(8,128)(2,1)S(1)}, s32[128,128]{1,0:T(8,128)S(1)}) custom-call(bf16[64,8192]{1,0:T(8,128)(2,1)} %bitcast.11, bf16[128,4096]{1,0:T(8,128)(2,1)} %inputs.1, s32[128,128]{1,0:T(8,128)} %words.1), custom_call_target="tpu_custom_call" | custom-call | flops 100000000 | bytes 4194304 | tf_op jit(solution)/shard_map/prepare/pallas_call | solution.py:84
  2.4 43.3 %all_to_all.15.grads = bf16[64,64,128]{2,1,0:T(8,128)(2,1)S(1)} all-to-all(bf16[64,64,128]{2,1,0:T(8,128)(2,1)S(1)} %get-tuple-element.11), channel_id=1, replica_groups={{37,38,39,40,41,42,43,44,45,46,47,48,49,50,51,52,53,54,55,56,57,58,59,6..., dimensions={0} | all-to-all | bytes 2097152 | tf_op jit(solution)/shard_map/all_to_all | solution.py:26
  45.6 0.6 token_sums.1
  46.3 0.0 copy-start
  46.3 12.3 %all_to_all.16 = f32[64,1,128]{2,1,0:T(1,128)S(1)} all-to-all(f32[64,1,128]{2,1,0:T(1,128)S(1)} %bitcast.8), channel_id=1, replica_groups={{37,38,39,40,41,42,43,44,45,46,47,48,49,50,51,52,53,54,55,56,57,58,59,6..., dimensions={0} | all-to-all | bytes 65536 | tf_op jit(solution)/shard_map/all_to_all | solution.py:26
  58.6 0.0 copy-done
  58.6 2.5 %middle.1 = (f32[12,1,128]{2,1,0:T(1,128)S(1)}, bf16[128,4096]{1,0:T(8,128)(2,1)}) custom-call(f32[64,128]{1,0:T(8,128)S(1)} %bitcast.7, bf16[64,64,128]{2,1,0:T(8,128)(2,1)S(1)} %all_to_all.15.grads, bf16[128,4096]{1,0:T(8,128)(2,1)S(1)} %get-tuple-element.14.inputs, s32[128,128]{1,0:T(8,128)S(1)} %get-tuple-element.15.words, ...), custom_call_target="tpu_custom_call" | custom-call | flops 100000000 | bytes 4194304 | tf_op jit(solution)/shard_map/middle/pallas_call | solution.py:187
  61.1 11.0 %all_to_all.17.parts = f32[12,1,128]{2,1,0:T(1,128)S(1)} all-to-all(f32[12,1,128]{2,1,0:T(1,128)S(1)} %get-tuple-element.16), channel_id=1, replica_groups={{576,640,704,0,64,128,192,256,320,384,448,512},{513,577,641,705,1,65,12..., dimensions={0} | all-to-all | bytes 12288 | tf_op jit(solution)/shard_map/all_to_all | solution.py:26
  72.1 0.6 last.1
Async XLA Ops:
  46.3 12.3 %copy-start = (f32[4096]{0:T(1024)S(1)}, f32[4096]{0:T(1024)}, u32[]{:S(2)}) copy-start(f32[4096]{0:T(1024)} %param.7) | copy-start | bytes 49156

commit v9 on v8

--- a/solution.py
+++ b/solution.py
@@ -18,7 +18,7 @@
 SHARES_ORDERS = [[(first + i) % 12 for i in range(12)] for first in FIRST_PLANES]
 SWAPPED = (3, 4, 5, 6, 9)
 CORES = 2
-EARLY = 4
+EARLY = 3
 F32 = jnp.float32
 
 
@@ -166,12 +166,14 @@
 
 
 def last_kernel(
-    order, norm, parts, grads, inputs, words, scale, gain, _, share, out, held, scaled, normed, factor, leave
+    order, norm, parts, grads, inputs, words, scale, gain, _, share, out, held, scaled, normed, factor, leave, mine, sem
 ):
     total = jnp.sum(parts[...], axis=0) * norm
     features = share.shape[1]
     first, second = total[:, :features], pltpu.roll(total, LANES - features, 1)[:, :features]
-    share[...] = jnp.where(lax.axis_index("ba") % CORES == 0, first, second)
+    mine[...] = jnp.where(lax.axis_index("ba") % CORES == 0, first, second)
+    share_copy = pltpu.make_async_copy(mine, share, sem)
+    share_copy.start()
 
     @pl.when(lax.axis_index("aa") >= EARLY)
     def _():
@@ -179,6 +181,8 @@
         copy = pltpu.make_async_copy(held, out, leave)
         copy.start()
         copy.wait()
+
+    share_copy.wait()
 
 
 def grad_call(kernel, operands, first_out, rows, width, aliased, name):
@@ -188,10 +192,11 @@
         kernel,
         out_shape=(first_out, jax.ShapeDtypeStruct((rows, width), jnp.bfloat16)),
         in_specs=[vmem] * (count - aliased) + [anywhere] * aliased,
-        out_specs=(vmem, anywhere),
+        out_specs=(anywhere if aliased else vmem, anywhere),
         scratch_shapes=[pltpu.VMEM((rows, width), jnp.bfloat16)]
         + [pltpu.VMEM((rows, width), F32)] * 3
-        + [pltpu.SemaphoreType.DMA],
+        + [pltpu.SemaphoreType.DMA]
+        + ([pltpu.VMEM(first_out.shape, F32), pltpu.SemaphoreType.DMA] if aliased else []),
         input_output_aliases={count - 1: 1} if aliased else {},
         compiler_params=params(14),
         cost_estimate=cost(10**8, 8 * rows * width),

time: 73 us -> 73 us (level)
  no operation moved by 1% of the time
where the time goes in v9:
time: 73 us; the launch traced here: 72.7 us
  blocking collectives  66.5 us (91%)
  Pallas kernels  5.49 us (8%)
    all_to_all x3, blocking collectives, exchange(): lax.all_to_all(parts, axis, 0, 0, tiled=True, axis_index_groups=groups)  66.5 us
    pallas_call x2, Pallas kernels, grad_call(): pl.pallas_call(kernel, out_shape=(first_out, jax.ShapeDtypeStruct((rows,...  3.13 us
    pallas_call x1, Pallas kernels, prepare(): pl.pallas_call(functools.partial(prepare_kernel, order), out_shape=(jax.S...  1.73 us

profile of v9, /device:TPU:1, one launch (start us, length us, event | category | flops | bytes accessed | tf_op | source)
XLA Modules:
  0.0 72.7 jit_solution(14055602002050620196)
XLA Ops:
  0.6 1.7 %prepare.1 = (bf16[64,64,128]{2,1,0:T(8,128)(2,1)S(1)}, bf16[64,64,128]{2,1,0:T(8,128)(2,1)S(1)}, f32[1,128]{1,0:T(1,128)S(1)}, bf16[128,4096]{1,0:T(8,128)(2,1)S(1)}, s32[128,128]{1,0:T(8,128)S(1)}) custom-call(bf16[64,8192]{1,0:T(8,128)(2,1)} %bitcast.11, bf16[128,4096]{1,0:T(8,128)(2,1)} %inputs.1, s32[128,128]{1,0:T(8,128)} %words.1), custom_call_target="tpu_custom_call" | custom-call | flops 100000000 | bytes 4194304 | tf_op jit(solution)/shard_map/prepare/pallas_call | solution.py:84
  2.4 43.3 %all_to_all.15.grads = bf16[64,64,128]{2,1,0:T(8,128)(2,1)S(1)} all-to-all(bf16[64,64,128]{2,1,0:T(8,128)(2,1)S(1)} %get-tuple-element.11), channel_id=1, replica_groups={{37,38,39,40,41,42,43,44,45,46,47,48,49,50,51,52,53,54,55,56,57,58,59,6..., dimensions={0} | all-to-all | bytes 2097152 | tf_op jit(solution)/shard_map/all_to_all | solution.py:26
  45.6 0.6 token_sums.1
  46.3 0.0 copy-start
  46.3 12.3 %all_to_all.16 = f32[64,1,128]{2,1,0:T(1,128)S(1)} all-to-all(f32[64,1,128]{2,1,0:T(1,128)S(1)} %bitcast.8), channel_id=1, replica_groups={{37,38,39,40,41,42,43,44,45,46,47,48,49,50,51,52,53,54,55,56,57,58,59,6..., dimensions={0} | all-to-all | bytes 65536 | tf_op jit(solution)/shard_map/all_to_all | solution.py:26
  58.6 0.0 copy-done
  58.6 2.5 %middle.1 = (f32[12,1,128]{2,1,0:T(1,128)S(1)}, bf16[128,4096]{1,0:T(8,128)(2,1)}) custom-call(f32[64,128]{1,0:T(8,128)S(1)} %bitcast.7, bf16[64,64,128]{2,1,0:T(8,128)(2,1)S(1)} %all_to_all.15.grads, bf16[128,4096]{1,0:T(8,128)(2,1)S(1)} %get-tuple-element.14.inputs, s32[128,128]{1,0:T(8,128)S(1)} %get-tuple-element.15.words, ...), custom_call_target="tpu_custom_call" | custom-call | flops 100000000 | bytes 4194304 | tf_op jit(solution)/shard_map/middle/pallas_call | solution.py:191
  61.1 11.0 %all_to_all.17.parts = f32[12,1,128]{2,1,0:T(1,128)S(1)} all-to-all(f32[12,1,128]{2,1,0:T(1,128)S(1)} %get-tuple-element.16), channel_id=1, replica_groups={{576,640,704,0,64,128,192,256,320,384,448,512},{513,577,641,705,1,65,12..., dimensions={0} | all-to-all | bytes 12288 | tf_op jit(solution)/shard_map/all_to_all | solution.py:26
  72.1 0.6 last.1
Async XLA Ops:
  46.3 12.3 %copy-start = (f32[4096]{0:T(1024)S(1)}, f32[4096]{0:T(1024)}, u32[]{:S(2)}) copy-start(f32[4096]{0:T(1024)} %param.7) | copy-start | bytes 49156
